TPU v7x, 32 devices: a whole 2x2x4 slice. The times are simulated.
32 devices in a mesh: fsdp: 8 (over z, x), dp: 4 (over y, core).
Axes of the slice: x: 2, y: 2, z: 4, core: 2. Of those that a mesh axis runs over, the one named last changes fastest.
Arguments:
- features: bfloat16 [8192, 1024], P(('fsdp', 'dp')), may hold values from -6 to 6
- normed: bfloat16 [8192, 4096], P(('fsdp', 'dp')), may hold values from -6 to 6
- relu_mask: int32 [8192, 4096], P(('fsdp', 'dp')), may hold values 0 or 1
- cotangent: bfloat16 [8192, 4096], P(('fsdp', 'dp')), may hold values from -40 to 40
- weight_shard: bfloat16 [1024, 4096], P('fsdp'), may hold values from -0.1875 to 0.1875
- norm_gain: float32 [4096], replicated, may hold values from 0.25 to 1.75
- inverse_deviation: float32 [4096], replicated, may hold values from 0.5 to 3
Outputs:
- grad_input: bfloat16 [8192, 1024], P(('fsdp', 'dp'))
- grad_weight: float32 [1024, 4096], P('fsdp')
- grad_gain: float32 [4096], replicated
- grad_shift: float32 [4096], replicated
All inputs are finite; a program needn't handle non-finite values. No bound on the sum of `relu_mask` on one device may be relied on, other than what follows from the above.
Results may differ from a plain program's by a relative error of at most 0.005.
Values may be sent and summed in bfloat16 or wider, within the bound.
No kernel may reach another device: no remote copies, remote signals or barrier semaphores. Data moves between devices by JAX's collectives and lax.ppermute only.
A program may use at most 128 MiB of HBM per device.

v0:
```python
import math

import jax
import jax.numpy as jnp
from jax import lax
from jax.sharding import PartitionSpec as P


def on_device(features, normed, relu_mask, cotangent, weight_shard, norm_gain, inverse_deviation):
    local_rows = features.shape[0]
    total_rows = local_rows * lax.axis_size("fsdp") * lax.axis_size("dp")
    masked = cotangent.astype(jnp.float32) * relu_mask.astype(jnp.float32)
    normed_f = normed.astype(jnp.float32)
    local_plain = jnp.sum(masked, axis=0)
    local_cross = jnp.sum(masked * normed_f, axis=0)
    sum_plain, sum_cross = lax.psum((local_plain, local_cross), ("fsdp", "dp"))
    norm_grad = (
        inverse_deviation
        * norm_gain
        * (masked - sum_plain / total_rows - normed_f * (sum_cross / total_rows))
    )
    norm_grad = norm_grad.astype(jnp.bfloat16)
    grad_input = lax.dot_general(
        norm_grad,
        lax.all_gather(weight_shard, "fsdp", axis=0, tiled=True),
        (((1,), (1,)), ((), ())),
        preferred_element_type=jnp.float32,
    ).astype(jnp.bfloat16)
    unit_block = lax.all_to_all(norm_grad, "dp", split_axis=1, concat_axis=0, tiled=True)
    unit_term = lax.dot_general(
        lax.all_gather(features, "dp", axis=0, tiled=True),
        unit_block,
        (((0,), (0,)), ((), ())),
        preferred_element_type=jnp.float32,
    )
    owner_part = lax.psum_scatter(unit_term, "fsdp", scatter_dimension=0, tiled=True)
    summed = lax.all_gather(owner_part, "dp", axis=1, tiled=True)
    rescale = 1.0 / math.sqrt(total_rows)
    return (grad_input, summed * rescale, sum_cross * rescale, sum_plain * rescale)


def solution(mesh):
    in_specs = (
        P(("fsdp", "dp"), None),
        P(("fsdp", "dp"), None),
        P(("fsdp", "dp"), None),
        P(("fsdp", "dp"), None),
        P("fsdp", None),
        P(),
        P(),
    )
    out_specs = (P(("fsdp", "dp"), None), P("fsdp", None), P(), P())
    return jax.shard_map(
        on_device, mesh=mesh, in_specs=in_specs, out_specs=out_specs, check_vma=False
    )
```

profile of v0, /device:TPU:0, one launch (start us, length us, event | category | flops | bytes accessed | tf_op | source)
XLA Modules:
  0.0 361.4 jit_solution(14963796621022647305)
XLA Ops:
  7.2 0.0 all-gather.6.cloned.1.call-start
  7.2 0.7 all-gather.6.cloned.1.call-update
  7.9 0.0 reduce-scatter.2.cloned.1.call-start
  7.9 3.3 copy.15
  11.2 5.6 %copy.14 = s32[256,4096]{0,1:T(8,128)} copy(s32[256,4096]{1,0:T(8,128)} %param.9) | data formatting | bytes 8388608 | tf_op args[2]
  16.8 4.1 %copy.13 = bf16[256,4096]{0,1:T(8,128)(2,1)} copy(bf16[256,4096]{1,0:T(8,128)(2,1)} %param.10) | data formatting | bytes 4194304 | tf_op args[3]
  21.0 0.0 copy-start.2
  21.0 0.0 copy-start.3
  21.0 4.1 %fusion.4 = (f32[4096]{0:T(1024)S(1)}, f32[4096]{0:T(1024)S(1)}) fusion(s32[256,4096]{0,1:T(8,128)} %copy.14, bf16[256,4096]{0,1:T(8,128)(2,1)} %copy.13, bf16[256,4096]{0,1:T(8,128)(2,1)S(1)} %copy.15), kind=kLoop, calls=%fused_computation.8 | loop fusion | flops 7331840 | bytes 8421376 | tf_op jit(solution)/shard_map/reduce_sum | solution.py:14
  25.1 0.0 copy-done.2
  25.1 0.0 copy-done.3
  25.1 42.3 %all-reduce = (f32[4096]{0:T(1024)S(1)}, f32[4096]{0:T(1024)S(1)}) all-reduce(f32[4096]{0:T(1024)S(1)} %get-tuple-element.17, f32[4096]{0:T(1024)S(1)} %get-tuple-element.16), channel_id=1, replica_groups=mesh['fsdp'=8,'dp'=4] {'fsdp','dp'}, use_global_device_ids=true, to_apply=%region_3.0 | all-reduce | flops 8192 | bytes 65536 | tf_op jit(solution)/shard_map/psum | solution.py:16
  67.4 0.6 broadcast_multiply_fusion.1
  68.0 4.3 %fusion.3 = bf16[256,4096]{0,1:T(8,128)(2,1)S(1)} fusion(bf16[256,4096]{0,1:T(8,128)(2,1)S(1)} %copy.15, f32[4096]{0:T(1024)S(1)} %get-tuple-element.24, f32[4096]{0:T(1024)S(1)} %get-tuple-element.21, f32[4096]{0:T(1024)S(1)} %mul.37, s32[256,4096]{0,1:T(8,128)} %copy.14, bf16[256,4096]{0,1:T(8,128)(2,1)} %copy.13), kind=kLoop, calls=%fused_computation.5 | loop fusion | flops 9437184 | bytes 10534912 | tf_op jit(solution)/shard_map/convert_element_type | solution.py:22
  72.3 0.0 copy-start
  72.3 29.0 %all_to_all.19 = bf16[256,4,1024]{0,2,1:T(8,128)(2,1)S(1)} all-to-all(bf16[256,4,1024]{0,2,1:T(8,128)(2,1)S(1)} %bitcast.9), channel_id=1, replica_groups=mesh['fsdp'=8,'dp'=4] {'dp'}, dimensions={1} | all-to-all | bytes 4194304 | tf_op jit(solution)/shard_map/all_to_all | solution.py:29
  101.3 0.0 copy-done
  101.3 2.4 copy.16
  103.7 0.0 all-gather.6.cloned.1.call-done
  103.7 6.5 %convolution_bitcast_fusion = f32[1024,1024]{0,1:T(8,128)} fusion(bf16[1024,1024]{1,0:T(8,128)(2,1)} %bitcast.11, bf16[1024,1024]{1,0:T(8,128)(2,1)} %all-gather.6.cloned.1.call-done), kind=kOutput, calls=%fused_computation.7 | convolution fusion | flops 2147483648 | bytes 8388608 | tf_op jit(solution)/shard_map/dot_general | solution.py:30
  110.3 0.0 reduce-scatter.2.cloned.1.call-update
  110.3 0.0 all-gather.8.cloned.1.call-start
  110.3 87.7 %reduce-scatter.2.cloned.1.call-done = f32[128,1024]{0,1:T(8,128)} async-done(((f32[1024,1024]{0,1:T(8,128)}), f32[128,1024]{0,1:T(8,128)}) %reduce-scatter.2.cloned.1.call-update) | async-done | bytes 524304 | tf_op jit(solution)/shard_map/reduce_scatter | solution.py:36
  198.0 0.0 all-gather.8.cloned.1.call-update
  198.1 0.0 all-gather.4.cloned.1.call-start
  198.1 0.5 all-gather.4.cloned.1.call-update
  198.6 23.2 %all-gather.8.cloned.1.call-done = f32[128,4096]{0,1:T(8,128)} async-done(((f32[128,1024]{0,1:T(8,128)}), f32[128,4096]{0,1:T(8,128)}) %all-gather.8.cloned.1.call-update) | async-done | bytes 2097168 | tf_op jit(solution)/shard_map/all_gather | solution.py:37
  221.8 3.1 broadcast_multiply_fusion
  224.9 3.0 copy.17
  227.9 120.4 %all-gather.4.cloned.1.call-done = bf16[1024,4096]{1,0:T(8,128)(2,1)} async-done(((bf16[128,4096]{1,0:T(8,128)(2,1)}), bf16[1024,4096]{1,0:T(8,128)(2,1)}) %all-gather.4.cloned.1.call-update) | async-done | bytes 8388624 | tf_op jit(solution)/shard_map/all_gather | solution.py:25
  348.3 0.0 copy-done.1
  348.3 6.6 %convolution_convert_fusion = bf16[256,1024]{1,0:T(8,128)(2,1)} fusion(bf16[256,4096]{0,1:T(8,128)(2,1)S(1)} %copy-done.1, bf16[1024,4096]{1,0:T(8,128)(2,1)} %all-gather.4.cloned.1.call-done), kind=kOutput, calls=%fused_computation.9 | convolution fusion | flops 2147745792 | bytes 11010048 | tf_op jit(solution)/shard_map/dot_general | solution.py:23
  (2 shorter events, 0.0 us)
Async XLA Ops:
  7.2 96.6 %all-gather.6.cloned.1.call-start = ((), (), s32[]{:S(2)}) async-start(), calls=%async_computation.3 | async-start | bytes 2621440 | tf_op jit(solution)/shard_map/all_gather | solution.py:31
  7.9 190.1 %reduce-scatter.2.cloned.1.call-start = ((), (), s32[]{:S(2)}) async-start(), calls=%async_computation.4 | async-start | bytes 4718592 | tf_op jit(solution)/shard_map/reduce_scatter | solution.py:36
  21.0 4.1 %copy-start.2 = (f32[4096]{0:T(1024)S(1)}, f32[4096]{0:T(1024)}, u32[]{:S(2)}) copy-start(f32[4096]{0:T(1024)} %param.13) | copy-start | bytes 49156
  21.0 4.1 %copy-start.3 = (f32[4096]{0:T(1024)S(1)}, f32[4096]{0:T(1024)}, u32[]{:S(2)}) copy-start(f32[4096]{0:T(1024)} %param.12) | copy-start | bytes 49156
  72.3 29.0 %copy-start = (bf16[256,4096]{0,1:T(8,128)(2,1)}, bf16[256,4096]{0,1:T(8,128)(2,1)S(1)}, u32[]{:S(2)}) copy-start(bf16[256,4096]{0,1:T(8,128)(2,1)S(1)} %fusion.3) | copy-start | bytes 6291460
  110.3 111.5 %all-gather.8.cloned.1.call-start = ((), (), s32[]{:S(2)}) async-start(), calls=%async_computation.5 | async-start | bytes 2621440 | tf_op jit(solution)/shard_map/all_gather | solution.py:37
  198.1 150.2 %all-gather.4.cloned.1.call-start = ((), (), s32[]{:S(2)}) async-start(), calls=%async_computation.2 | async-start | bytes 9437184 | tf_op jit(solution)/shard_map/all_gather | solution.py:25
  224.9 123.4 %copy-start.1 = (bf16[256,4096]{0,1:T(8,128)(2,1)S(1)}, bf16[256,4096]{0,1:T(8,128)(2,1)}, u32[]{:S(2)}) copy-start(bf16[256,4096]{0,1:T(8,128)(2,1)} %copy-done) | copy-start | bytes 6291460
Sparse Core Ops, SparseCore 0:
  9.5 25.2 all-gather.5
  110.4 87.5 reduce-scatter.1
  199.6 22.1 all-gather.7
  223.8 124.4 all-gather.3
where the time goes:
time: 362 us; the launch traced here: 361 us
  waiting for transfers between devices  232 us (64%)
  blocking collectives  71.3 us (20%)
  local copies, waits for them, and re-layouts  18.4 us (5%)
  between operations  13.8 us (4%)
  matrix products  13.1 us (4%)
  other arithmetic  12.1 us (3%)
    all_gather x1, waiting for transfers between devices, on_device(): lax.all_gather(weight_shard, 'fsdp', axis=0, tiled=True)  120 us
    reduce_scatter x1, waiting for transfers between devices, on_device(): lax.psum_scatter(unit_term, 'fsdp', scatter_dimension=0, tiled=True)  87.7 us
    psum x1, blocking collectives, on_device(): sum_plain, sum_cross = lax.psum((local_plain, local_cross), ('fsdp', 'dp'))  42.3 us
    all_to_all x1, blocking collectives, on_device(): lax.all_to_all(norm_grad, 'dp', split_axis=1, concat_axis=0, tiled=True)  29 us
    all_gather x1, waiting for transfers between devices, on_device(): summed = lax.all_gather(owner_part, 'dp', axis=1, tiled=True)  23.2 us
    unnamed x12, local copies, waits for them, and re-layouts  16.1 us
  transfers between devices with their start and end apart: 4, of which 3 were waited for; matrix products, arithmetic and copies ran while one was open for 8% of the time, Pallas kernels for 0%

commit v1 on v0

v1 whole, which is shorter than its diff:
```python
import functools
import math

import jax
import jax.numpy as jnp
from jax import lax
from jax.experimental import pallas as pl
from jax.experimental.pallas import tpu as pltpu
from jax.sharding import PartitionSpec as P

F32 = jnp.float32
BF16 = jnp.bfloat16


def swap(x, axis, bit):
    size = lax.axis_size(axis)
    return lax.ppermute(x, axis, [(i, i ^ bit) for i in range(size)])


def bits_of(size):
    return [1 << b for b in range(size.bit_length() - 1)]


def column_blocks(columns):
    width = 512
    while columns % width:
        width //= 2
    return width


def sums_kernel(cot_ref, mask_ref, normed_ref, masked_ref, sums_ref):
    masked = cot_ref[...].astype(F32) * mask_ref[...].astype(F32)
    masked_ref[...] = masked.astype(BF16)
    sums_ref[0:1, :] = jnp.sum(masked, axis=0, keepdims=True)
    sums_ref[1:2, :] = jnp.sum(masked * normed_ref[...].astype(F32), axis=0, keepdims=True)


def local_sums(cotangent, relu_mask, normed):
    rows, units = cotangent.shape
    width = column_blocks(units)
    spec = pl.BlockSpec((rows, width), lambda i: (0, i))
    return pl.pallas_call(
        sums_kernel,
        grid=(units // width,),
        in_specs=[spec, spec, spec],
        out_specs=[spec, pl.BlockSpec((2, width), lambda i: (0, i))],
        out_shape=[
            jax.ShapeDtypeStruct((rows, units), BF16),
            jax.ShapeDtypeStruct((2, units), F32),
        ],
        cost_estimate=pl.CostEstimate(flops=8 * rows * units, bytes_accessed=10 * rows * units, transcendentals=0),
        name="local_sums",
    )(cotangent, relu_mask, normed)


def grad_kernel(total_rows, order_ref, masked_ref, normed_ref, sums_ref, scale_ref, out_ref):
    mean_plain = sums_ref[0:1, :] / total_rows
    mean_cross = sums_ref[1:2, :] / total_rows
    scale = scale_ref[0:1, :] * scale_ref[1:2, :]
    value = scale * (
        masked_ref[...].astype(F32) - mean_plain - normed_ref[...].astype(F32) * mean_cross
    )
    out_ref[0] = value.astype(BF16)


def norm_grad_blocks(order, masked, normed, sums, scales, parts, total_rows):
    rows, units = masked.shape
    width = units // parts
    wide = pl.BlockSpec((rows, width), lambda i, order: (0, order[i]))
    thin = pl.BlockSpec((2, width), lambda i, order: (0, order[i]))
    return pl.pallas_call(
        functools.partial(grad_kernel, total_rows),
        grid_spec=pltpu.PrefetchScalarGridSpec(
            num_scalar_prefetch=1,
            grid=(parts,),
            in_specs=[wide, wide, thin, thin],
            out_specs=pl.BlockSpec((1, rows, width), lambda i, order: (i, 0, 0)),
        ),
        out_shape=jax.ShapeDtypeStruct((parts, rows, width), BF16),
        cost_estimate=pl.CostEstimate(flops=8 * rows * units, bytes_accessed=6 * rows * units, transcendentals=0),
        name="norm_grad",
    )(order, masked, normed, sums, scales)


def place_kernel(rescale, order_ref, part_ref, out_ref):
    out_ref[...] = part_ref[0].astype(F32) * rescale


def place_units(order, pieces, rescale):
    parts, rows, width = pieces.shape
    return pl.pallas_call(
        functools.partial(place_kernel, rescale),
        grid_spec=pltpu.PrefetchScalarGridSpec(
            num_scalar_prefetch=1,
            grid=(parts,),
            in_specs=[pl.BlockSpec((1, rows, width), lambda i, order: (i, 0, 0))],
            out_specs=pl.BlockSpec((rows, width), lambda i, order: (0, order[i])),
        ),
        out_shape=jax.ShapeDtypeStruct((rows, parts * width), F32),
        cost_estimate=pl.CostEstimate(flops=rows * parts * width, bytes_accessed=6 * rows * parts * width, transcendentals=0),
        name="place_units",
    )(order, pieces)


def reversed_bits(values, bits):
    out = values * 0
    for place, bit in enumerate(bits):
        out = out + ((values // bit) % 2) * bits[len(bits) - 1 - place]
    return out


def on_device(features, normed, relu_mask, cotangent, weight_shard, norm_gain, inverse_deviation):
    rows, inputs = features.shape
    units = normed.shape[1]
    fsdp, dp = lax.axis_size("fsdp"), lax.axis_size("dp")
    total_rows = rows * fsdp * dp
    width = units // dp
    f, d = lax.axis_index("fsdp"), lax.axis_index("dp")
    dp_bits, fsdp_bits = bits_of(dp), bits_of(fsdp)
    dp_place = reversed_bits(jnp.arange(dp, dtype=jnp.int32), dp_bits)
    order = jnp.bitwise_xor(d.astype(jnp.int32), dp_place)

    weight = lax.dynamic_slice_in_dim(weight_shard, d * width, width, axis=1)[None]
    for bit in reversed(fsdp_bits):
        weight = jnp.concatenate([weight, swap(weight, "fsdp", bit)], axis=0)
    weight_place = reversed_bits(jnp.bitwise_xor(f, jnp.arange(fsdp, dtype=jnp.int32)), fsdp_bits)
    weight = jnp.take(weight, weight_place, axis=0, mode="clip").reshape(inputs, width)

    group = features[None]
    for bit in reversed(dp_bits):
        group = jnp.concatenate([group, swap(group, "dp", bit)], axis=0)

    masked, own_sums = local_sums(cotangent, relu_mask, normed)
    everyone = ("fsdp", "dp")
    spread = own_sums.reshape(fsdp * dp, -1)
    spread = lax.all_to_all(spread, everyone, split_axis=0, concat_axis=0, tiled=True)
    owned = jnp.sum(spread, axis=0, keepdims=True)
    spread = jnp.broadcast_to(owned, spread.shape)
    spread = lax.all_to_all(spread, everyone, split_axis=0, concat_axis=0, tiled=True)
    sums = spread.reshape(2, units)

    scales = jnp.stack([inverse_deviation, norm_gain])
    blocks = norm_grad_blocks(order, masked, normed, sums, scales, dp, total_rows)

    blocks = blocks.reshape((2,) * len(dp_bits) + (rows, width))
    for axis, bit in reversed(list(enumerate(dp_bits))):
        away = lax.index_in_dim(blocks, 1, axis, keepdims=True)
        here = lax.index_in_dim(blocks, 0, axis, keepdims=True)
        blocks = jnp.concatenate([here, swap(away, "dp", bit)], axis=axis)
    grads = blocks.reshape(dp * rows, width)

    term = lax.dot_general(
        group.reshape(dp * rows, inputs), grads, (((0,), (0,)), ((), ())), preferred_element_type=F32
    ).astype(BF16)
    part = lax.dot_general(
        grads, weight, (((1,), (1,)), ((), ())), preferred_element_type=F32
    ).reshape((2,) * len(dp_bits) + (rows, inputs))

    term = lax.all_to_all(
        term.reshape(fsdp, inputs // fsdp, width), "fsdp", split_axis=0, concat_axis=0, tiled=True
    )
    pieces = jnp.sum(term.astype(F32), axis=0).astype(BF16)[None]
    for bit in reversed(dp_bits):
        pieces = jnp.concatenate([pieces, swap(pieces, "dp", bit)], axis=0)
    rescale = 1.0 / math.sqrt(total_rows)
    grad_weight = place_units(order, pieces, rescale)

    for bit in dp_bits:
        part = part[0] + swap(part[1].astype(BF16), "dp", bit).astype(F32)
    return (part.astype(BF16), grad_weight, sums[1] * rescale, sums[0] * rescale)


def solution(mesh):
    rows = P(("fsdp", "dp"), None)
    return jax.shard_map(
        on_device,
        mesh=mesh,
        in_specs=(rows, rows, rows, rows, P("fsdp", None), P(), P()),
        out_specs=(rows, P("fsdp", None), P(), P()),
        check_vma=False,
    )
```

time: 362 us -> 198 us (0.55)
  waiting for transfers between devices: 232 us -> 124 us
  blocking collectives: 71.3 us -> 0 us
  starting transfers between devices: 0.16 us -> 20.3 us
  Pallas kernels: 0 us -> 16.8 us
  between operations: 13.8 us -> 0.81 us
  local copies, waits for them, and re-layouts: 18.4 us -> 10.5 us
  other arithmetic: 12.1 us -> 17.1 us
  matrix products: 13.1 us -> 8.37 us
    all_gather x3 -> x0, waiting for transfers between devices: 144 us -> none  [the longest x1 120 us: on_device(): lax.all_gather(weight_shard, 'fsdp', axis=0, tiled=True)]
    ppermute x0 -> x11, waiting for transfers between devices: none -> 110 us  [swap(): return lax.ppermute(x, axis, [(i, i ^ bit) for i in range(size)])]
    reduce_scatter x1 -> x0, waiting for transfers between devices: 87.7 us -> none  [on_device(): lax.psum_scatter(unit_term, 'fsdp', scatter_dimension=0, tiled=True)]
    psum x1 -> x0, blocking collectives: 42.3 us -> none  [on_device(): sum_plain, sum_cross = lax.psum((local_plain, local_cross), ('fsdp', 'dp'))]
    all_to_all x1 -> x0, blocking collectives: 29 us -> none  [on_device(): lax.all_to_all(norm_grad, 'dp', split_axis=1, concat_axis=0, tiled=True)]
    pallas_call x0 -> x3, Pallas kernels: none -> 16.8 us  [the longest x1 7.3 us: local_sums(): pl.pallas_call(sums_kernel, grid=(units // width,), in_specs=[spec, spec,...]
    unnamed x12 -> x14, local copies, waits for them, and re-layouts: 16.1 us -> 0.73 us
    all_to_all x0 -> x3, starting transfers between devices: none -> 13.6 us  [the longest x2 9.89 us: on_device(): lax.all_to_all(spread, everyone, split_axis=0, concat_axis=0, tiled=True)]
  transfers between devices with their start and end apart: 4 -> 14, of which waited for: 3 -> 9; matrix products, arithmetic and copies ran while one was open for 8% -> 15% of each run, Pallas kernels for 0% -> 0%
where the time goes in v1:
time: 198 us; the launch traced here: 197 us
  waiting for transfers between devices  124 us (63%)
  starting transfers between devices  20.3 us (10%)
  other arithmetic  17.1 us (9%)
  Pallas kernels  16.8 us (8%)
  local copies, waits for them, and re-layouts  10.5 us (5%)
  matrix products  8.37 us (4%)
    ppermute x11, waiting for transfers between devices, swap(): return lax.ppermute(x, axis, [(i, i ^ bit) for i in range(size)])  110 us
    all_to_all x2, waiting for transfers between devices, on_device(): lax.all_to_all(spread, everyone, split_axis=0, concat_axis=0, tiled=True)  13.3 us
    all_to_all x2, starting transfers between devices, on_device(): lax.all_to_all(spread, everyone, split_axis=0, concat_axis=0, tiled=True)  9.89 us
    pallas_call x1, Pallas kernels, local_sums(): pl.pallas_call(sums_kernel, grid=(units // width,), in_specs=[spec, spec,...  7.3 us
    ppermute x11, starting transfers between devices, swap(): return lax.ppermute(x, axis, [(i, i ^ bit) for i in range(size)])  6.66 us
    concatenate x3, other arithmetic, on_device(): weight = jnp.concatenate([weight, swap(weight, 'fsdp', bit)], axis=0)  5.96 us
    pallas_call x1, Pallas kernels, norm_grad_blocks(): pl.pallas_call(functools.partial(grad_kernel, total_rows), grid_spec=pltp...  5.25 us
    dot_general x1, matrix products, on_device(): lax.dot_general(grads, weight, (((1,), (1,)), ((), ())), preferred_elemen...  4.59 us
  transfers between devices with their start and end apart: 14, of which 9 were waited for; matrix products, arithmetic and copies ran while one was open for 15% of the time, Pallas kernels for 0%

profile of v1, /device:TPU:0, one launch (start us, length us, event | category | flops | bytes accessed | tf_op | source)
XLA Modules:
  0.0 197.4 jit_solution(11281737259953874572)
XLA Ops:
  0.7 7.3 %local_sums.1 = (bf16[256,4096]{1,0:T(8,128)(2,1)}, f32[2,4096]{1,0:T(2,128)}) custom-call(bf16[256,4096]{1,0:T(8,128)(2,1)} %cot_ref.1, s32[256,4096]{1,0:T(8,128)} %mask_ref.1, bf16[256,4096]{1,0:T(8,128)(2,1)} %normed_ref.3), custom_call_target="tpu_custom_call" | custom-call | flops 8388608 | bytes 10485760 | tf_op jit(solution)/shard_map/local_sums/pallas_call | solution.py:42
  8.0 1.4 all_to_all.17
  9.4 7.3 %all-to-all-start = ((f32[32,1,256]{2,1,0:T(1,128)}), f32[32,1,256]{2,1,0:T(1,128)S(1)}, u32[]{:S(2)}, u32[]{:S(2)}) async-start(f32[32,1,256]{2,1,0:T(1,128)} %all_to_all.17), calls=%async_computation | async-start | bytes 65536 | tf_op jit(solution)/shard_map/all_to_all | solution.py:136
  17.4 6.6 %all-to-all-done = f32[32,1,256]{2,1,0:T(1,128)S(1)} async-done(((f32[32,1,256]{2,1,0:T(1,128)}), f32[32,1,256]{2,1,0:T(1,128)S(1)}, u32[]{:S(2)}, u32[]{:S(2)}) %all-to-all-start) | async-done | bytes 32800 | tf_op jit(solution)/shard_map/all_to_all | solution.py:136
  24.7 2.6 %all-to-all-start.1 = ((f32[32,1,256]{2,1,0:T(1,128)}), f32[32,1,256]{2,1,0:T(1,128)S(1)}, u32[]{:S(2)}, u32[]{:S(2)}) async-start(f32[32,1,256]{2,1,0:T(1,128)} %broadcast_in_dim.17), calls=%async_computation.1 | async-start | bytes 65536 | tf_op jit(solution)/shard_map/all_to_all | solution.py:139
  27.8 6.7 %all-to-all-done.1 = f32[32,1,256]{2,1,0:T(1,128)S(1)} async-done(((f32[32,1,256]{2,1,0:T(1,128)}), f32[32,1,256]{2,1,0:T(1,128)S(1)}, u32[]{:S(2)}, u32[]{:S(2)}) %all-to-all-start.1) | async-done | bytes 32800 | tf_op jit(solution)/shard_map/all_to_all | solution.py:139
  35.2 5.3 %norm_grad.1 = bf16[4,256,1024]{2,1,0:T(8,128)(2,1)} custom-call(s32[4]{0:T(128)} %fusion.7.order_ref, bf16[256,4096]{1,0:T(8,128)(2,1)} %get-tuple-element.6.masked_ref, bf16[256,4096]{1,0:T(8,128)(2,1)} %normed_ref.3, f32[2,4096]{1,0:T(2,128)} %reshape.235.sums_ref, f32[2,4096]{1,0:T(2,128)} %pad_maximum_fusion.9.scale_ref), custom_call_target="tpu_custom_call" | custom-call | flops 8388608 | bytes 6291456 | tf_op jit(solution)/shard_map/norm_grad/pallas_call | solution.py:71
  40.5 1.8 fusion.15
  42.8 1.5 collective-permute-start.7
  44.3 34.4 %collective-permute-done.7 = bf16[1,256,1024]{2,1,0:T(8,128)(2,1)S(1)} collective-permute-done((bf16[1,256,1024]{2,1,0:T(8,128)(2,1)S(1)}, bf16[1,256,1024]{2,1,0:T(8,128)(2,1)S(1)}, u32[]{:S(2)}, u32[]{:S(2)}) %collective-permute-start.7) | collective-permute-done | bytes 524320 | tf_op jit(solution)/shard_map/ppermute | solution.py:17
  78.7 1.1 pad_maximum_fusion.5
  79.8 1.2 fusion
  81.7 14.1 %collective-permute-done.2 = bf16[1,128,1024]{2,1,0:T(8,128)(2,1)S(1)} collective-permute-done((bf16[1,128,1024]{2,1,0:T(8,128)(2,1)S(1)}, bf16[1,128,1024]{2,1,0:T(8,128)(2,1)S(1)}, u32[]{:S(2)}, u32[]{:S(2)}) %collective-permute-start.2) | collective-permute-done | bytes 262176 | tf_op jit(solution)/shard_map/ppermute | solution.py:17
  97.4 1.4 pad_maximum_fusion.2
  98.8 1.4 pad_maximum_fusion
  100.3 3.8 %convolution_convert_fusion = bf16[1024,1024]{1,0:T(8,128)(2,1)} fusion(bf16[1024,1024]{1,0:T(8,128)(2,1)S(1)} %bitcast.37, bf16[1024,1024]{1,0:T(8,128)(2,1)S(1)} %bitcast.35), kind=kOutput, calls=%fused_computation.8 | convolution fusion | flops 2148532224 | bytes 6291456 | tf_op jit(solution)/shard_map/dot_general | solution.py:152
  104.1 3.7 %all-to-all-start.2 = ((bf16[8,128,1024]{2,1,0:T(8,128)(2,1)}), bf16[8,128,1024]{2,1,0:T(8,128)(2,1)S(1)}, u32[]{:S(2)}, u32[]{:S(2)}) async-start(bf16[8,128,1024]{2,1,0:T(8,128)(2,1)} %bitcast.34), calls=%async_computation.2 | async-start | bytes 4194304 | tf_op jit(solution)/shard_map/all_to_all | solution.py:159
  107.8 4.7 %collective-permute-done.3 = bf16[2,128,1024]{2,1,0:T(8,128)(2,1)} collective-permute-done((bf16[2,128,1024]{2,1,0:T(8,128)(2,1)}, bf16[2,128,1024]{2,1,0:T(8,128)(2,1)}, u32[]{:S(2)}, u32[]{:S(2)}) %collective-permute-start.3) | collective-permute-done | bytes 524320 | tf_op jit(solution)/shard_map/ppermute | solution.py:17
  112.5 2.2 %pad_maximum_fusion.4 = bf16[4,128,1024]{2,1,0:T(8,128)(2,1)} fusion(bf16[2,128,1024]{2,1,0:T(8,128)(2,1)} %collective-permute-done.3, bf16[1,128,1024]{2,1,0:T(8,128)(2,1)} %copy-done.2, bf16[1,128,1024]{2,1,0:T(8,128)(2,1)S(1)} %dynamic-slice_bitcast_fusion), kind=kLoop, calls=%fused_computation.15 | loop fusion | flops 1048576 | bytes 2097152 | tf_op jit(solution)/shard_map/concatenate | solution.py:125
  114.7 1.5 collective-permute-start.4
  116.3 39.2 %collective-permute-done.4 = bf16[4,128,1024]{2,1,0:T(8,128)(2,1)} collective-permute-done((bf16[4,128,1024]{2,1,0:T(8,128)(2,1)}, bf16[4,128,1024]{2,1,0:T(8,128)(2,1)}, u32[]{:S(2)}, u32[]{:S(2)}) %collective-permute-start.4) | collective-permute-done | bytes 1048608 | tf_op jit(solution)/shard_map/ppermute | solution.py:17
  155.4 2.9 %pad_maximum_fusion.1 = bf16[8,128,1024]{2,1,0:T(8,128)(2,1)} fusion(bf16[4,128,1024]{2,1,0:T(8,128)(2,1)} %collective-permute-done.4, bf16[2,128,1024]{2,1,0:T(8,128)(2,1)} %collective-permute-done.3, bf16[1,128,1024]{2,1,0:T(8,128)(2,1)} %copy-done.2, bf16[1,128,1024]{2,1,0:T(8,128)(2,1)S(1)} %dynamic-slice_bitcast_fusion), kind=kLoop, calls=%fused_computation.5 | loop fusion | flops 3145728 | bytes 4194304 | tf_op jit(solution)/shard_map/concatenate | solution.py:125
  158.4 3.6 %gather_fusion = bf16[8,128,1024]{2,1,0:T(8,128)(2,1)} fusion(bf16[8,128,1024]{2,1,0:T(8,128)(2,1)} %pad_maximum_fusion.1, s32[1024]{0:T(1024)S(1)} %pad_clamp_fusion), kind=kCustom, calls=%fused_computation | custom fusion | bytes 4194336 | tf_op jit(solution)/shard_map/jit(_take)/gather | solution.py:127
  162.0 4.6 %fusion.16 = f32[1024,1024]{1,0:T(8,128)S(1)} fusion(bf16[1024,1024]{1,0:T(8,128)(2,1)} %bitcast.36, bf16[1024,1024]{1,0:T(8,128)(2,1)} %bitcast.38), kind=kOutput, calls=%fused_computation.60 | convolution fusion | flops 2147483648 | bytes 8388608 | tf_op jit(solution)/shard_map/dot_general | solution.py:155
  167.1 2.4 %collective-permute-done.5 = bf16[2,256,1024]{2,1,0:T(8,128)(2,1)S(1)} collective-permute-done((bf16[2,256,1024]{2,1,0:T(8,128)(2,1)S(1)}, bf16[2,256,1024]{2,1,0:T(8,128)(2,1)S(1)}, u32[]{:S(2)}, u32[]{:S(2)}) %collective-permute-start.5) | collective-permute-done | bytes 1048608 | tf_op jit(solution)/shard_map/ppermute | solution.py:17
  169.5 1.6 convert_add_fusion
  172.5 1.3 fusion.3
  173.8 1.2 collective-permute-start.6
  175.0 5.8 %collective-permute-done.9 = bf16[1,128,1024]{2,1,0:T(8,128)(2,1)S(1)} collective-permute-done((bf16[1,128,1024]{2,1,0:T(8,128)(2,1)S(1)}, bf16[1,128,1024]{2,1,0:T(8,128)(2,1)S(1)}, u32[]{:S(2)}, u32[]{:S(2)}) %collective-permute-start.9) | collective-permute-done | bytes 262176 | tf_op jit(solution)/shard_map/ppermute | solution.py:17
  181.5 9.6 %collective-permute-done.6 = bf16[256,1024]{1,0:T(8,128)(2,1)S(1)} collective-permute-done((bf16[256,1024]{1,0:T(8,128)(2,1)S(1)}, bf16[256,1024]{1,0:T(8,128)(2,1)S(1)}, u32[]{:S(2)}, u32[]{:S(2)}) %collective-permute-start.6) | collective-permute-done | bytes 524320 | tf_op jit(solution)/shard_map/ppermute | solution.py:17
  192.1 1.1 pad_maximum_fusion.6.part_ref
  193.2 4.3 %place_units.1 = f32[128,4096]{1,0:T(8,128)} custom-call(s32[4]{0:T(128)} %fusion.7.order_ref, bf16[4,128,1024]{2,1,0:T(8,128)(2,1)} %pad_maximum_fusion.6.part_ref), custom_call_target="tpu_custom_call" | custom-call | flops 524288 | bytes 3145728 | tf_op jit(solution)/shard_map/place_units/pallas_call | solution.py:91
  (43 shorter events, 9.0 us)
Async XLA Ops:
  0.6 80.8 %copy-start = (bf16[128,4096]{1,0:T(8,128)(2,1)S(1)}, bf16[128,4096]{1,0:T(8,128)(2,1)}, u32[]{:S(2)}) copy-start(bf16[128,4096]{1,0:T(8,128)(2,1)} %param.11) | copy-start | bytes 3145732
  0.6 16.1 %copy-start.5 = (f32[4096]{0:T(1024)S(1)}, f32[4096]{0:T(1024)}, u32[]{:S(2)}) copy-start(f32[4096]{0:T(1024)} %param.12) | copy-start | bytes 49156
  0.7 16.1 %copy-start.6 = (f32[4096]{0:T(1024)S(1)}, f32[4096]{0:T(1024)}, u32[]{:S(2)}) copy-start(f32[4096]{0:T(1024)} %param.13) | copy-start | bytes 49156
  9.4 14.6 %all-to-all-start = ((f32[32,1,256]{2,1,0:T(1,128)}), f32[32,1,256]{2,1,0:T(1,128)S(1)}, u32[]{:S(2)}, u32[]{:S(2)}) async-start(f32[32,1,256]{2,1,0:T(1,128)} %all_to_all.17), calls=%async_computation | async-start | bytes 65536 | tf_op jit(solution)/shard_map/all_to_all | solution.py:136
  24.7 9.8 %all-to-all-start.1 = ((f32[32,1,256]{2,1,0:T(1,128)}), f32[32,1,256]{2,1,0:T(1,128)S(1)}, u32[]{:S(2)}, u32[]{:S(2)}) async-start(f32[32,1,256]{2,1,0:T(1,128)} %broadcast_in_dim.17), calls=%async_computation.1 | async-start | bytes 65536 | tf_op jit(solution)/shard_map/all_to_all | solution.py:139
  40.5 2.3 %copy-start.4 = (bf16[256,1024]{1,0:T(8,128)(2,1)S(1)}, bf16[256,1024]{1,0:T(8,128)(2,1)}, u32[]{:S(2)}) copy-start(bf16[256,1024]{1,0:T(8,128)(2,1)} %param.7) | copy-start | bytes 1572868
  42.2 37.6 %collective-permute-start = (bf16[2,1,256,1024]{3,2,1,0:T(8,128)(2,1)S(1)}, bf16[2,1,256,1024]{3,2,1,0:T(8,128)(2,1)S(1)}, u32[]{:S(2)}, u32[]{:S(2)}) collective-permute-start(bf16[2,1,256,1024]{3,2,1,0:T(8,128)(2,1)S(1)} %get-tuple-element.11), channel_id=1, source_target_pairs={{0,2},{1,3},{2,0},{3,1},{4,6},{5,7},{6,4},{7,5},{8,10},{9,11},{10,... | collective-permute-start | bytes 3145736 | tf_op jit(solution)/shard_map/ppermute | solution.py:17
  42.8 35.9 %collective-permute-start.7 = (bf16[1,256,1024]{2,1,0:T(8,128)(2,1)S(1)}, bf16[1,256,1024]{2,1,0:T(8,128)(2,1)S(1)}, u32[]{:S(2)}, u32[]{:S(2)}) collective-permute-start(bf16[1,256,1024]{2,1,0:T(8,128)(2,1)S(1)} %bitcast.39), channel_id=1, source_target_pairs={{0,2},{1,3},{2,0},{3,1},{4,6},{5,7},{6,4},{7,5},{8,10},{9,11},{10,... | collective-permute-start | bytes 1572872 | tf_op jit(solution)/shard_map/ppermute | solution.py:17
  79.8 17.6 %collective-permute-start.8 = (bf16[2,256,1024]{2,1,0:T(8,128)(2,1)}, bf16[2,256,1024]{2,1,0:T(8,128)(2,1)}, u32[]{:S(2)}, u32[]{:S(2)}) collective-permute-start(bf16[2,256,1024]{2,1,0:T(8,128)(2,1)} %pad_maximum_fusion.5), channel_id=1, source_target_pairs={{0,1},{1,0},{2,3},{3,2},{4,5},{5,4},{6,7},{7,6},{8,9},{9,8},{10,11... | collective-permute-start | bytes 3145736 | tf_op jit(solution)/shard_map/ppermute | solution.py:17
  81.0 17.9 %collective-permute-start.1 = (bf16[1,2,256,1024]{3,2,1,0:T(8,128)(2,1)}, bf16[1,2,256,1024]{3,2,1,0:T(8,128)(2,1)}, u32[]{:S(2)}, u32[]{:S(2)}) collective-permute-start(bf16[1,2,256,1024]{3,2,1,0:T(8,128)(2,1)} %get-tuple-element.9), channel_id=1, source_target_pairs={{0,1},{1,0},{2,3},{3,2},{4,5},{5,4},{6,7},{7,6},{8,9},{9,8},{10,11... | collective-permute-start | bytes 3145736 | tf_op jit(solution)/shard_map/ppermute | solution.py:17
  81.5 14.4 %collective-permute-start.2 = (bf16[1,128,1024]{2,1,0:T(8,128)(2,1)S(1)}, bf16[1,128,1024]{2,1,0:T(8,128)(2,1)S(1)}, u32[]{:S(2)}, u32[]{:S(2)}) collective-permute-start(bf16[1,128,1024]{2,1,0:T(8,128)(2,1)S(1)} %dynamic-slice_bitcast_fusion), channel_id=1, source_target_pairs={{0,16},{4,20},{8,24},{12,28},{16,0},{20,4},{24,8},{28,12},{1,17},{... | collective-permute-start | bytes 786440 | tf_op jit(solution)/shard_map/ppermute | solution.py:17
  95.9 0.7 copy-start.2
  97.4 15.1 %collective-permute-start.3 = (bf16[2,128,1024]{2,1,0:T(8,128)(2,1)}, bf16[2,128,1024]{2,1,0:T(8,128)(2,1)}, u32[]{:S(2)}, u32[]{:S(2)}) collective-permute-start(bf16[2,128,1024]{2,1,0:T(8,128)(2,1)} %pad_maximum_fusion.7), channel_id=1, source_target_pairs={{0,8},{4,12},{8,0},{12,4},{16,24},{20,28},{24,16},{28,20},{1,9},{5... | collective-permute-start | bytes 1572872 | tf_op jit(solution)/shard_map/ppermute | solution.py:17
  100.3 3.8 %copy-start.3 = (bf16[2,2,256,1024]{3,2,1,0:T(8,128)(2,1)}, bf16[2,2,256,1024]{3,2,1,0:T(8,128)(2,1)S(1)}, u32[]{:S(2)}) copy-start(bf16[2,2,256,1024]{3,2,1,0:T(8,128)(2,1)S(1)} %pad_maximum_fusion) | copy-start | bytes 6291460
  104.1 67.1 %all-to-all-start.2 = ((bf16[8,128,1024]{2,1,0:T(8,128)(2,1)}), bf16[8,128,1024]{2,1,0:T(8,128)(2,1)S(1)}, u32[]{:S(2)}, u32[]{:S(2)}) async-start(bf16[8,128,1024]{2,1,0:T(8,128)(2,1)} %bitcast.34), calls=%async_computation.2 | async-start | bytes 4194304 | tf_op jit(solution)/shard_map/all_to_all | solution.py:159
  114.7 40.8 %collective-permute-start.4 = (bf16[4,128,1024]{2,1,0:T(8,128)(2,1)}, bf16[4,128,1024]{2,1,0:T(8,128)(2,1)}, u32[]{:S(2)}, u32[]{:S(2)}) collective-permute-start(bf16[4,128,1024]{2,1,0:T(8,128)(2,1)} %pad_maximum_fusion.4), channel_id=1, source_target_pairs={{0,4},{4,0},{8,12},{12,8},{16,20},{20,16},{24,28},{28,24},{1,5},{5... | collective-permute-start | bytes 3145736 | tf_op jit(solution)/shard_map/ppermute | solution.py:17
  166.8 2.7 %collective-permute-start.5 = (bf16[2,256,1024]{2,1,0:T(8,128)(2,1)S(1)}, bf16[2,256,1024]{2,1,0:T(8,128)(2,1)S(1)}, u32[]{:S(2)}, u32[]{:S(2)}) collective-permute-start(bf16[2,256,1024]{2,1,0:T(8,128)(2,1)S(1)} %bitcast.42), channel_id=1, source_target_pairs={{0,1},{1,0},{2,3},{3,2},{4,5},{5,4},{6,7},{7,6},{8,9},{9,8},{10,11... | collective-permute-start | bytes 3145736 | tf_op jit(solution)/shard_map/ppermute | solution.py:17
  171.5 19.7 %copy-start.1 = (f32[2,256,1024]{2,1,0:T(8,128)S(1)}, f32[2,256,1024]{2,1,0:T(8,128)}, u32[]{:S(2)}) copy-start(f32[2,256,1024]{2,1,0:T(8,128)} %convert_add_fusion) | copy-start | bytes 6291460
  171.5 9.2 %collective-permute-start.9 = (bf16[1,128,1024]{2,1,0:T(8,128)(2,1)S(1)}, bf16[1,128,1024]{2,1,0:T(8,128)(2,1)S(1)}, u32[]{:S(2)}, u32[]{:S(2)}) collective-permute-start(bf16[1,128,1024]{2,1,0:T(8,128)(2,1)S(1)} %bitcast.31), channel_id=1, source_target_pairs={{0,2},{1,3},{2,0},{3,1},{4,6},{5,7},{6,4},{7,5},{8,10},{9,11},{10,... | collective-permute-start | bytes 786440 | tf_op jit(solution)/shard_map/ppermute | solution.py:17
  173.8 17.4 %collective-permute-start.6 = (bf16[256,1024]{1,0:T(8,128)(2,1)S(1)}, bf16[256,1024]{1,0:T(8,128)(2,1)S(1)}, u32[]{:S(2)}, u32[]{:S(2)}) collective-permute-start(bf16[256,1024]{1,0:T(8,128)(2,1)S(1)} %fusion.3), channel_id=1, source_target_pairs={{0,2},{1,3},{2,0},{3,1},{4,6},{5,7},{6,4},{7,5},{8,10},{9,11},{10,... | collective-permute-start | bytes 1572872 | tf_op jit(solution)/shard_map/ppermute | solution.py:17
  180.8 11.3 %collective-permute-start.10 = (bf16[2,128,1024]{2,1,0:T(8,128)(2,1)S(1)}, bf16[2,128,1024]{2,1,0:T(8,128)(2,1)S(1)}, u32[]{:S(2)}, u32[]{:S(2)}) collective-permute-start(bf16[2,128,1024]{2,1,0:T(8,128)(2,1)S(1)} %pad_maximum_fusion.8), channel_id=1, source_target_pairs={{0,1},{1,0},{2,3},{3,2},{4,5},{5,4},{6,7},{7,6},{8,9},{9,8},{10,11... | collective-permute-start | bytes 1572872 | tf_op jit(solution)/shard_map/ppermute | solution.py:17

commit v2 on v1

v2 whole, which is shorter than its diff:
```python
import functools
import math

import jax
import jax.numpy as jnp
from jax import lax
from jax.experimental import pallas as pl
from jax.experimental.pallas import tpu as pltpu
from jax.sharding import PartitionSpec as P


F32 = jnp.float32
BF16 = jnp.bfloat16


def swap(x, axis, offset):
    size = lax.axis_size(axis)
    return lax.ppermute(x, axis, [(i, i ^ offset) for i in range(size)])


def bits_of(size):
    return [1 << b for b in range(size.bit_length() - 1)]


def offsets(bits):
    found = [0]
    for bit in bits:
        found = found + [offset ^ bit for offset in found]
    return found


def cost(flops, moved):
    return pl.CostEstimate(flops=flops, bytes_accessed=moved, transcendentals=0)


def sums_kernel(cot_ref, mask_ref, normed_ref, masked_ref, sums_ref, total_ref):
    step, last = pl.program_id(0), pl.num_programs(0) - 1
    rows, units = cot_ref.shape
    tiles = units // 128

    @pl.when(step == 0)
    def _():
        total_ref[...] = jnp.zeros_like(total_ref)

    for tile in range(tiles):
        columns = slice(tile * 128, tile * 128 + 128)
        masked = cot_ref[:, columns].astype(F32) * mask_ref[:, columns].astype(F32)
        masked_ref[:, columns] = masked.astype(BF16)
        cross = masked * normed_ref[:, columns].astype(F32)
        total_ref[0, :, columns] += jnp.sum(masked.reshape(rows // 8, 8, 128), axis=0)
        total_ref[1, :, columns] += jnp.sum(cross.reshape(rows // 8, 8, 128), axis=0)

    @pl.when(step == last)
    def _():
        for tile in range(tiles):
            columns = slice(tile * 128, tile * 128 + 128)
            for which in range(2):
                sums_ref[which * tiles + tile] = jnp.sum(
                    total_ref[which, :, columns], axis=0, keepdims=True
                )


def local_sums(cotangent, relu_mask, normed):
    rows, units = cotangent.shape
    depth = 64
    spec = pl.BlockSpec((depth, units), lambda i: (i, 0))
    lines = 2 * units // 128
    return pl.pallas_call(
        sums_kernel,
        grid=(rows // depth,),
        in_specs=[spec, spec, spec],
        out_specs=[spec, pl.BlockSpec((lines, 1, 128), lambda i: (0, 0, 0))],
        out_shape=[
            jax.ShapeDtypeStruct((rows, units), BF16),
            jax.ShapeDtypeStruct((lines, 1, 128), F32),
        ],
        scratch_shapes=[pltpu.VMEM((2, 8, units), F32)],
        cost_estimate=cost(8 * rows * units, 10 * rows * units),
        name="local_sums",
    )(cotangent, relu_mask, normed)


def grad_kernel(total_rows, block_ref, masked_ref, normed_ref, plain_ref, cross_ref, inverse_ref, gain_ref, *outs):
    for at, out_ref in enumerate(outs):

        @pl.when(pl.program_id(0) == at)
        def _():
            for tile in range(out_ref.shape[1] // 128):
                columns = slice(tile * 128, tile * 128 + 128)
                mean_plain = plain_ref[tile] / total_rows
                mean_cross = cross_ref[tile] / total_rows
                scale = inverse_ref[tile] * gain_ref[tile]
                value = scale * (
                    masked_ref[:, columns].astype(F32)
                    - mean_plain
                    - normed_ref[:, columns].astype(F32) * mean_cross
                )
                out_ref[:, columns] = value.astype(BF16)


def norm_grads(blocks, masked, normed, sums, inverse, gain, width, total_rows):
    rows, units = masked.shape
    lines = width // 128
    wide = pl.BlockSpec((rows, width), lambda i, block: (0, block[i]))
    thin = pl.BlockSpec((lines, 1, 128), lambda i, block: (block[i], 0, 0))
    later = pl.BlockSpec((lines, 1, 128), lambda i, block: (units // width + block[i], 0, 0))
    count = len(blocks)
    return pl.pallas_call(
        functools.partial(grad_kernel, total_rows),
        grid_spec=pltpu.PrefetchScalarGridSpec(
            num_scalar_prefetch=1,
            grid=(count,),
            in_specs=[wide, wide, thin, later, thin, thin],
            out_specs=[pl.BlockSpec((rows, width), lambda i, block: (0, 0))] * count,
        ),
        out_shape=[jax.ShapeDtypeStruct((rows, width), BF16)] * count,
        cost_estimate=cost(8 * count * rows * width, 6 * count * rows * width),
        name="norm_grad",
    )(jnp.stack(blocks), masked, normed, sums, sums, inverse, gain)


def term_kernel(parts, order_ref, *refs):
    away_ref, kept_ref = refs[-2:]
    grads = refs[2 * parts : 3 * parts]
    for out_ref, rows in ((away_ref, refs[:parts]), (kept_ref, refs[parts : 2 * parts])):
        total = 0.0
        for row_ref, grad_ref in zip(rows, grads):
            total = total + lax.dot_general(
                row_ref[...], grad_ref[...], (((0,), (0,)), ((), ())), preferred_element_type=F32
            )
        out_ref[0] = total.astype(out_ref.dtype)


def weight_term(order, group, grads, blocks):
    rows, inputs = group[0].shape
    width = grads[0].shape[1]
    deep = inputs // blocks
    half, parts = blocks // 2, len(group)
    if deep % 128:
        total = 0.0
        for row, grad in zip(group, grads):
            total = total + lax.dot_general(
                row, grad, (((0,), (0,)), ((), ())), preferred_element_type=F32
            )
        total = jnp.take(total.reshape(blocks, deep, width), order, axis=0, mode="clip")
        return total[:half].astype(BF16), total[half:]
    away = pl.BlockSpec((rows, deep), lambda i, order: (0, order[i]))
    kept = pl.BlockSpec((rows, deep), lambda i, order: (0, order[half + i]))
    whole = pl.BlockSpec((rows, width), lambda i, order: (0, 0))
    out = pl.BlockSpec((1, deep, width), lambda i, order: (i, 0, 0))
    return pl.pallas_call(
        functools.partial(term_kernel, parts),
        grid_spec=pltpu.PrefetchScalarGridSpec(
            num_scalar_prefetch=1,
            grid=(half,),
            in_specs=[away] * parts + [kept] * parts + [whole] * parts,
            out_specs=[out, out],
        ),
        out_shape=[
            jax.ShapeDtypeStruct((half, deep, width), BF16),
            jax.ShapeDtypeStruct((half, deep, width), F32),
        ],
        cost_estimate=cost(2 * parts * rows * inputs * width, 5 * inputs * width + 4 * parts * rows * inputs),
        name="weight_term",
    )(order, *group, *group, *grads)


def rows_kernel(chunks, steps, order_ref, *refs):
    away_ref, kept_ref = refs[-2:]
    grads = refs[len(steps) : -2]
    parts = len(grads) // chunks
    half = parts // 2
    first = 0
    for weight_ref, count in zip(refs, steps):

        @pl.when(jnp.logical_and(pl.program_id(0) >= first, pl.program_id(0) < first + count))
        def _():
            blocks, deep, units = weight_ref.shape
            weight = weight_ref[...].reshape(blocks * deep, units)
            width = units // chunks
            for part in range(parts):
                total = 0.0
                for chunk in range(chunks):
                    total = total + lax.dot_general(
                        grads[part * chunks + chunk][...],
                        weight[:, chunk * width : (chunk + 1) * width],
                        (((1,), (1,)), ((), ())),
                        preferred_element_type=F32,
                    )
                out_ref = kept_ref if part < half else away_ref
                for block in range(blocks):
                    place = order_ref[pl.program_id(0) * blocks + block]
                    columns = pl.ds(pl.multiple_of(place * deep, deep), deep)
                    out_ref[part % half, :, columns] = total[
                        :, block * deep : (block + 1) * deep
                    ].astype(out_ref.dtype)

        first += count


def input_terms(order, weights, grads):
    parts, chunks = len(grads), len(grads[0])
    rows, width = grads[0][0].shape
    deep, units = weights[0].shape[1:]
    blocks = 2 if deep < 256 else 1
    steps = [weight.shape[0] // blocks for weight in weights]
    specs, first = [], 0
    for count in steps:
        specs.append(
            pl.BlockSpec(
                (blocks, deep, units),
                lambda i, order, first=first, count=count: (jnp.clip(i - first, 0, count - 1), 0, 0),
            )
        )
        first += count
    inputs = order.shape[0] * deep
    flat = [piece for part in grads for piece in part]
    whole = pl.BlockSpec((rows, width), lambda i, order: (0, 0))
    out = pl.BlockSpec((parts // 2, rows, inputs), lambda i, order: (0, 0, 0))
    return pl.pallas_call(
        functools.partial(rows_kernel, chunks, steps),
        grid_spec=pltpu.PrefetchScalarGridSpec(
            num_scalar_prefetch=1,
            grid=(sum(steps),),
            in_specs=specs + [whole] * len(flat),
            out_specs=[out, out],
        ),
        out_shape=[
            jax.ShapeDtypeStruct((parts // 2, rows, inputs), BF16),
            jax.ShapeDtypeStruct((parts // 2, rows, inputs), F32),
        ],
        cost_estimate=cost(2 * parts * rows * inputs * units, 3 * parts * rows * inputs + 2 * inputs * units),
        name="input_terms",
    )(order, *weights, *flat)


def place_kernel(rescale, chunks, order_ref, *refs):
    out_ref = refs[-1]
    parts = (len(refs) - 1) // chunks
    width = out_ref.shape[1] // chunks
    for part in range(parts):

        @pl.when(pl.program_id(0) == part)
        def _():
            for chunk in range(chunks):
                piece = refs[part * chunks + chunk][...]
                out_ref[:, chunk * width : (chunk + 1) * width] = piece.astype(F32) * rescale


def place_units(order, pieces, rescale):
    parts, chunks = len(pieces), len(pieces[0])
    rows, width = pieces[0][0].shape
    flat = [piece for part in pieces for piece in part]
    return pl.pallas_call(
        functools.partial(place_kernel, rescale, chunks),
        grid_spec=pltpu.PrefetchScalarGridSpec(
            num_scalar_prefetch=1,
            grid=(parts,),
            in_specs=[pl.BlockSpec((rows, width), lambda i, order: (0, 0))] * len(flat),
            out_specs=pl.BlockSpec((rows, chunks * width), lambda i, order: (0, order[i])),
        ),
        out_shape=jax.ShapeDtypeStruct((rows, parts * chunks * width), F32),
        cost_estimate=cost(rows * parts * chunks * width, 6 * rows * parts * chunks * width),
        name="place_units",
    )(order, *flat)


def everyones_sum(own):
    everyone = ("fsdp", "dp")
    parts = lax.axis_size("fsdp") * lax.axis_size("dp")
    lines = own.shape[0]
    spread = own if lines % parts == 0 else own.reshape(parts, 1, -1)
    size = spread.shape[0] // parts
    spread = lax.all_to_all(spread, everyone, split_axis=0, concat_axis=0, tiled=True)
    owned = jnp.sum(spread.reshape(parts, size, 1, -1), axis=0, keepdims=True)
    spread = jnp.broadcast_to(owned, (parts,) + owned.shape[1:]).reshape(spread.shape)
    spread = lax.all_to_all(spread, everyone, split_axis=0, concat_axis=0, tiled=True)
    return spread.reshape(own.shape)


def chunks_of(width):
    return 2 if width % 256 == 0 else 1


def on_device(features, normed, relu_mask, cotangent, weight_shard, norm_gain, inverse_deviation):
    rows, inputs = features.shape
    units = normed.shape[1]
    fsdp, dp = lax.axis_size("fsdp"), lax.axis_size("dp")
    total_rows = rows * fsdp * dp
    width = units // dp
    chunks = chunks_of(width)
    part_width = width // chunks
    f, d = lax.axis_index("fsdp"), lax.axis_index("dp")
    f, d = f.astype(jnp.int32), d.astype(jnp.int32)
    dp_bits, fsdp_bits = bits_of(dp), bits_of(fsdp)
    partners = list(range(dp))
    deep = inputs // fsdp

    weight_bits = fsdp_bits[-1:] + fsdp_bits[:-1]
    weight = lax.dynamic_slice_in_dim(weight_shard, d * width, width, axis=1)[None]
    for at, bit in enumerate(weight_bits):
        came = swap(weight, "fsdp", bit)
        if at < len(weight_bits) - 1:
            weight = jnp.concatenate([weight, came], axis=0)
    input_order = jnp.bitwise_xor(f, jnp.array(offsets(weight_bits), jnp.int32))
    weights = [weight, came]
    if deep % 128:
        weight = jnp.concatenate(weights, axis=0)
        back = jnp.zeros_like(input_order).at[input_order].set(jnp.arange(fsdp, dtype=jnp.int32))
        weights = [jnp.take(weight, back, axis=0, mode="clip").reshape(inputs // 128, 128, width)]
        input_order = jnp.arange(inputs // 128, dtype=jnp.int32)

    group = {0: features}
    for bit in reversed(dp_bits):
        for k in list(group):
            group[k ^ bit] = swap(group[k], "dp", bit)

    masked, own_sums = local_sums(cotangent, relu_mask, normed)
    sums = everyones_sum(own_sums)
    lined = lambda vector: vector.reshape(-1, 1, 128)

    grads = [{} for _ in range(chunks)]
    near = [k for k in partners if k < dp // 2]
    far = [k for k in reversed(partners) if k >= dp // 2]
    turns = [[(chunk, k) for k in far] for chunk in range(chunks)]
    turns.append([(chunk, k) for chunk in range(chunks) for k in reversed(near)])
    for turn in turns:
        blocks = [jnp.bitwise_xor(d, k) * chunks + chunk for chunk, k in turn]
        pieces = norm_grads(
            blocks, masked, normed, sums, lined(inverse_deviation), lined(norm_gain),
            part_width, total_rows,
        )
        for (chunk, k), piece in zip(turn, pieces):
            grads[chunk][k] = swap(piece, "dp", k) if k else piece

    places = offsets(list(reversed(fsdp_bits)))
    term_order = jnp.bitwise_xor(f, jnp.array(places[fsdp // 2 :] + places[: fsdp // 2], jnp.int32))
    finished = []
    for chunk in range(chunks):
        away, kept = weight_term(
            term_order, [group[k] for k in partners],
            [grads[chunk][k] for k in partners], fsdp,
        )
        for bit in fsdp_bits:
            came = swap(away, "fsdp", bit)
            half = kept.shape[0] // 2
            if half:
                away = (kept[half:] + came[half:].astype(F32)).astype(BF16)
                kept = kept[:half] + came[:half].astype(F32)
            else:
                kept = kept + came.astype(F32)
        pieces = {0: kept.reshape(deep, part_width).astype(BF16)}
        for bit in reversed(dp_bits):
            for k in list(pieces):
                pieces[k ^ bit] = swap(pieces[k], "dp", bit)
        finished.append(pieces)
    rescale = 1.0 / math.sqrt(total_rows)
    unit_order = jnp.bitwise_xor(d, jnp.arange(dp, dtype=jnp.int32))
    grad_weight = place_units(
        unit_order, [[finished[c][k] for c in range(chunks)] for k in partners], rescale
    )

    places = offsets(list(reversed(dp_bits)))
    away, kept = input_terms(
        input_order, weights, [[grads[c][k] for c in range(chunks)] for k in places]
    )
    for bit in dp_bits:
        came = swap(away, "dp", bit)
        half = kept.shape[0] // 2
        if half:
            away = (kept[half:] + came[half:].astype(F32)).astype(BF16)
            kept = kept[:half] + came[:half].astype(F32)
        else:
            kept = kept + came.astype(F32)
    sums = sums.reshape(2, units) * rescale
    return (kept.reshape(rows, inputs).astype(BF16), grad_weight, sums[1], sums[0])


def solution(mesh):
    rows = P(("fsdp", "dp"), None)
    return jax.shard_map(
        on_device,
        mesh=mesh,
        in_specs=(rows, rows, rows, rows, P("fsdp", None), P(), P()),
        out_specs=(rows, P("fsdp", None), P(), P()),
        check_vma=False,
    )
```

time: 198 us -> 143 us (0.72)
  waiting for transfers between devices: 124 us -> 51.8 us
  Pallas kernels: 16.8 us -> 39.1 us
  starting transfers between devices: 20.3 us -> 29.3 us
  matrix products: 8.37 us -> 0 us
  local copies, waits for them, and re-layouts: 10.5 us -> 6.75 us
  other arithmetic: 17.1 us -> 14.4 us
    ppermute x11 -> x26, waiting for transfers between devices: 110 us -> 37.9 us  [swap(): return lax.ppermute(x, axis, [(i, i ^ offset) for i in range(size)])]
    pallas_call x3 -> x8, Pallas kernels: 16.8 us -> 39.1 us  [the longest x2 11.6 us: weight_term(): pl.pallas_call(functools.partial(term_kernel, parts), grid_spec=pltpu.Pre...]
    ppermute x11 -> x26, starting transfers between devices: 6.66 us -> 21.9 us  [swap(): return lax.ppermute(x, axis, [(i, i ^ offset) for i in range(size)])]
    concatenate x9 -> x2, other arithmetic: 12.2 us -> 3.06 us  [on_device(): weight = jnp.concatenate([weight, came], axis=0)]
    dot_general x2 -> x0, matrix products: 8.37 us -> none  [the longest x1 4.59 us: on_device(): lax.dot_general(grads, weight, (((1,), (1,)), ((), ())), preferred_elemen...]
    convert_element_type x1 -> x8, other arithmetic: 0.94 us -> 7.83 us  [the longest x5 4.6 us: on_device(): away = (kept[half:] + came[half:].astype(F32)).astype(BF16)]
    all_to_all x3 -> x2, starting transfers between devices: 13.6 us -> 7.37 us  [everyones_sum(): lax.all_to_all(spread, everyone, split_axis=0, concat_axis=0, tiled=True)]
    unnamed x14 -> x46, local copies, waits for them, and re-layouts: 0.73 us -> 5.45 us
  transfers between devices with their start and end apart: 14 -> 28, of which waited for: 9 -> 11; matrix products, arithmetic and copies ran while one was open for 15% -> 9% of each run, Pallas kernels for 0% -> 27%
where the time goes in v2:
time: 143 us; the launch traced here: 142 us
  waiting for transfers between devices  51.8 us (36%)
  Pallas kernels  39.1 us (27%)
  starting transfers between devices  29.3 us (20%)
  other arithmetic  14.4 us (10%)
  local copies, waits for them, and re-layouts  6.75 us (5%)
    ppermute x26, waiting for transfers between devices, swap(): return lax.ppermute(x, axis, [(i, i ^ offset) for i in range(size)])  37.9 us
    ppermute x26, starting transfers between devices, swap(): return lax.ppermute(x, axis, [(i, i ^ offset) for i in range(size)])  21.9 us
    all_to_all x2, waiting for transfers between devices, everyones_sum(): lax.all_to_all(spread, everyone, split_axis=0, concat_axis=0, tiled=True)  13.9 us
    pallas_call x2, Pallas kernels, weight_term(): pl.pallas_call(functools.partial(term_kernel, parts), grid_spec=pltpu.Pre...  11.6 us
    pallas_call x3, Pallas kernels, norm_grads(): pl.pallas_call(functools.partial(grad_kernel, total_rows), grid_spec=pltp...  10.3 us
    pallas_call x1, Pallas kernels, input_terms(): pl.pallas_call(functools.partial(rows_kernel, chunks, steps), grid_spec=p...  7.84 us
    all_to_all x2, starting transfers between devices, everyones_sum(): lax.all_to_all(spread, everyone, split_axis=0, concat_axis=0, tiled=True)  7.37 us
    pallas_call x1, Pallas kernels, local_sums(): pl.pallas_call(sums_kernel, grid=(rows // depth,), in_specs=[spec, spec,...  5.57 us
  transfers between devices with their start and end apart: 28, of which 11 were waited for; matrix products, arithmetic and copies ran while one was open for 9% of the time, Pallas kernels for 27%

profile of v2, /device:TPU:0, one launch (start us, length us, event | category | flops | bytes accessed | tf_op | source)
XLA Modules:
  0.0 142.2 jit_solution(11931943278261441467)
XLA Ops:
  0.7 1.2 copy-done
  1.9 4.1 %collective-permute-start = (bf16[1,128,1024]{2,1,0:T(8,128)(2,1)S(1)}, bf16[1,128,1024]{2,1,0:T(8,128)(2,1)S(1)}, u32[]{:S(2)}, u32[]{:S(2)}) collective-permute-start(bf16[1,128,1024]{2,1,0:T(8,128)(2,1)S(1)} %dynamic-slice_bitcast_fusion), channel_id=1, source_target_pairs={{0,16},{4,20},{8,24},{12,28},{16,0},{20,4},{24,8},{28,12},{1,17},{... | collective-permute-start | bytes 786440 | tf_op jit(solution)/shard_map/ppermute | solution.py:18
  6.0 1.5 %collective-permute-start.12 = (bf16[256,1024]{1,0:T(8,128)(2,1)}, bf16[256,1024]{1,0:T(8,128)(2,1)S(1)}, u32[]{:S(2)}, u32[]{:S(2)}) collective-permute-start(bf16[256,1024]{1,0:T(8,128)(2,1)} %refs_4_.3), channel_id=1, source_target_pairs={{0,2},{1,3},{2,0},{3,1},{4,6},{5,7},{6,4},{7,5},{8,10},{9,11},{10,... | collective-permute-start | bytes 1572872 | tf_op jit(solution)/shard_map/ppermute | solution.py:18
  7.5 10.4 %collective-permute-done = bf16[1,128,1024]{2,1,0:T(8,128)(2,1)S(1)} collective-permute-done((bf16[1,128,1024]{2,1,0:T(8,128)(2,1)S(1)}, bf16[1,128,1024]{2,1,0:T(8,128)(2,1)S(1)}, u32[]{:S(2)}, u32[]{:S(2)}) %collective-permute-start) | collective-permute-done | bytes 262176 | tf_op jit(solution)/shard_map/ppermute | solution.py:18
  19.5 1.5 %collective-permute-start.1 = (bf16[2,128,1024]{2,1,0:T(8,128)(2,1)}, bf16[2,128,1024]{2,1,0:T(8,128)(2,1)}, u32[]{:S(2)}, u32[]{:S(2)}) collective-permute-start(bf16[2,128,1024]{2,1,0:T(8,128)(2,1)} %pad_maximum_fusion.1), channel_id=1, source_target_pairs={{0,4},{4,0},{8,12},{12,8},{16,20},{20,16},{24,28},{28,24},{1,5},{5... | collective-permute-start | bytes 1572872 | tf_op jit(solution)/shard_map/ppermute | solution.py:18
  21.0 5.6 %local_sums.1 = (bf16[256,4096]{1,0:T(8,128)(2,1)}, f32[64,1,128]{2,1,0:T(1,128)}) custom-call(bf16[256,4096]{1,0:T(8,128)(2,1)} %cot_ref.1, s32[256,4096]{1,0:T(8,128)} %mask_ref.1, bf16[256,4096]{1,0:T(8,128)(2,1)} %normed_ref.7), custom_call_target="tpu_custom_call" | custom-call | flops 8388608 | bytes 10485760 | tf_op jit(solution)/shard_map/local_sums/pallas_call | solution.py:68
  26.6 4.8 %all-to-all-start = ((f32[64,1,128]{2,1,0:T(1,128)}), f32[64,1,128]{2,1,0:T(1,128)S(1)}, u32[]{:S(2)}, u32[]{:S(2)}) async-start(f32[64,1,128]{2,1,0:T(1,128)} %get-tuple-element.21), calls=%async_computation | async-start | bytes 65536 | tf_op jit(solution)/shard_map/all_to_all | solution.py:274
  31.4 7.2 %all-to-all-done = f32[64,1,128]{2,1,0:T(1,128)S(1)} async-done(((f32[64,1,128]{2,1,0:T(1,128)}), f32[64,1,128]{2,1,0:T(1,128)S(1)}, u32[]{:S(2)}, u32[]{:S(2)}) %all-to-all-start) | async-done | bytes 32800 | tf_op jit(solution)/shard_map/all_to_all | solution.py:274
  39.3 2.6 %all-to-all-start.1 = ((f32[64,1,128]{2,1,0:T(1,128)}), f32[64,1,128]{2,1,0:T(1,128)S(1)}, u32[]{:S(2)}, u32[]{:S(2)}) async-start(f32[64,1,128]{2,1,0:T(1,128)} %bitcast.6), calls=%async_computation.1 | async-start | bytes 65536 | tf_op jit(solution)/shard_map/all_to_all | solution.py:277
  42.5 6.7 %all-to-all-done.1.plain_ref.cross_ref = f32[64,1,128]{2,1,0:T(1,128)S(1)} async-done(((f32[64,1,128]{2,1,0:T(1,128)}), f32[64,1,128]{2,1,0:T(1,128)S(1)}, u32[]{:S(2)}, u32[]{:S(2)}) %all-to-all-start.1) | async-done | bytes 32800 | tf_op jit(solution)/shard_map/all_to_all | solution.py:277
  49.8 3.0 %norm_grad.4 = (bf16[256,512]{1,0:T(8,128)(2,1)}, bf16[256,512]{1,0:T(8,128)(2,1)}) custom-call(s32[2]{0:T(128)} %pad_add_fusion.1.block_ref, bf16[256,4096]{1,0:T(8,128)(2,1)} %get-tuple-element.20.masked_ref, bf16[256,4096]{1,0:T(8,128)(2,1)} %normed_ref.7, f32[64,1,128]{2,1,0:T(1,128)} %copy-done.5, f32[64,1,128]{2,1,0:T(1,128)} %copy-done.5, ...), custom_call_target="tpu_custom_call" | custom-call | flops 2097152 | bytes 1572864 | tf_op jit(solution)/shard_map/norm_grad/pallas_call | solution.py:108
  54.5 4.4 %norm_grad.3 = (bf16[256,512]{1,0:T(8,128)(2,1)}, bf16[256,512]{1,0:T(8,128)(2,1)}, bf16[256,512]{1,0:T(8,128)(2,1)}, bf16[256,512]{1,0:T(8,128)(2,1)}) custom-call(s32[4]{0:T(128)} %pad_add_fusion.block_ref, bf16[256,4096]{1,0:T(8,128)(2,1)} %get-tuple-element.20.masked_ref, bf16[256,4096]{1,0:T(8,128)(2,1)} %normed_ref.7, f32[64,1,128]{2,1,0:T(1,128)} %copy-done.5, ...), custom_call_target="tpu_custom_call" | custom-call | flops 4194304 | bytes 3145728 | tf_op jit(solution)/shard_map/norm_grad/pallas_call | solution.py:108
  59.0 1.6 %collective-permute-start.7 = (bf16[256,512]{1,0:T(8,128)(2,1)}, bf16[256,512]{1,0:T(8,128)(2,1)}, u32[]{:S(2)}, u32[]{:S(2)}) collective-permute-start(bf16[256,512]{1,0:T(8,128)(2,1)} %get-tuple-element.28), channel_id=1, source_target_pairs={{0,3},{1,2},{2,1},{3,0},{4,7},{5,6},{6,5},{7,4},{8,11},{9,10},{10,... | collective-permute-start | bytes 786440 | tf_op jit(solution)/shard_map/ppermute | solution.py:18
  60.6 2.2 %pad_maximum_fusion.refs_0_ = bf16[4,128,1024]{2,1,0:T(8,128)(2,1)} fusion(bf16[2,128,1024]{2,1,0:T(8,128)(2,1)} %collective-permute-done.1, bf16[1,128,1024]{2,1,0:T(8,128)(2,1)} %copy-done.11, bf16[1,128,1024]{2,1,0:T(8,128)(2,1)S(1)} %dynamic-slice_bitcast_fusion), kind=kLoop, calls=%fused_computation | loop fusion | flops 1048576 | bytes 2097152 | tf_op jit(solution)/shard_map/concatenate | solution.py:304
  64.5 2.9 %norm_grad.5 = (bf16[256,512]{1,0:T(8,128)(2,1)}, bf16[256,512]{1,0:T(8,128)(2,1)}) custom-call(s32[2]{0:T(128)} %pad_add_fusion.2.block_ref, bf16[256,4096]{1,0:T(8,128)(2,1)} %get-tuple-element.20.masked_ref, bf16[256,4096]{1,0:T(8,128)(2,1)} %normed_ref.7, f32[64,1,128]{2,1,0:T(1,128)} %copy-done.5, f32[64,1,128]{2,1,0:T(1,128)} %copy-done.5, ...), custom_call_target="tpu_custom_call" | custom-call | flops 2097152 | bytes 1572864 | tf_op jit(solution)/shard_map/norm_grad/pallas_call | solution.py:108
  68.0 1.6 %collective-permute-start.8 = (bf16[256,512]{1,0:T(8,128)(2,1)}, bf16[256,512]{1,0:T(8,128)(2,1)S(1)}, u32[]{:S(2)}, u32[]{:S(2)}) collective-permute-start(bf16[256,512]{1,0:T(8,128)(2,1)} %get-tuple-element.29), channel_id=1, source_target_pairs={{0,3},{1,2},{2,1},{3,0},{4,7},{5,6},{6,5},{7,4},{8,11},{9,10},{10,... | collective-permute-start | bytes 786440 | tf_op jit(solution)/shard_map/ppermute | solution.py:18
  70.4 5.7 %weight_term.2 = (bf16[4,128,512]{2,1,0:T(8,128)(2,1)}, f32[4,128,512]{2,1,0:T(8,128)}) custom-call(s32[8]{0:T(128)} %broadcast_xor_fusion.order_ref, bf16[256,1024]{1,0:T(8,128)(2,1)} %refs_4_.3, bf16[256,1024]{1,0:T(8,128)(2,1)} %copy-done.3, bf16[256,1024]{1,0:T(8,128)(2,1)} %copy-done.2, bf16[256,1024]{1,0:T(8,128)(2,1)} %copy-done.4, ...), custom_call_target="tpu_custom_call" | custom-call | flops 1073741824 | bytes 6815744 | tf_op jit(solution)/shard_map/weight_term/pallas_call | solution.py:151
  76.9 3.3 %collective-permute-done.8.refs_9_.refs_11_ = bf16[256,512]{1,0:T(8,128)(2,1)S(1)} collective-permute-done((bf16[256,512]{1,0:T(8,128)(2,1)}, bf16[256,512]{1,0:T(8,128)(2,1)S(1)}, u32[]{:S(2)}, u32[]{:S(2)}) %collective-permute-start.8) | collective-permute-done | bytes 262176 | tf_op jit(solution)/shard_map/ppermute | solution.py:18
  80.9 5.9 %weight_term.3 = (bf16[4,128,512]{2,1,0:T(8,128)(2,1)}, f32[4,128,512]{2,1,0:T(8,128)}) custom-call(s32[8]{0:T(128)} %broadcast_xor_fusion.order_ref, bf16[256,1024]{1,0:T(8,128)(2,1)} %refs_4_.3, bf16[256,1024]{1,0:T(8,128)(2,1)} %copy-done.3, bf16[256,1024]{1,0:T(8,128)(2,1)} %copy-done.2, bf16[256,1024]{1,0:T(8,128)(2,1)} %copy-done.4, ...), custom_call_target="tpu_custom_call" | custom-call | flops 1073741824 | bytes 6815744 | tf_op jit(solution)/shard_map/weight_term/pallas_call | solution.py:151
  87.9 2.4 %collective-permute-done.14 = bf16[4,128,512]{2,1,0:T(8,128)(2,1)S(1)} collective-permute-done((bf16[4,128,512]{2,1,0:T(8,128)(2,1)}, bf16[4,128,512]{2,1,0:T(8,128)(2,1)S(1)}, u32[]{:S(2)}, u32[]{:S(2)}) %collective-permute-start.14) | collective-permute-done | bytes 524320 | tf_op jit(solution)/shard_map/ppermute | solution.py:18
  91.3 1.4 %collective-permute-start.15 = (bf16[2,128,512]{2,1,0:T(8,128)(2,1)S(1)}, bf16[2,128,512]{2,1,0:T(8,128)(2,1)}, u32[]{:S(2)}, u32[]{:S(2)}) collective-permute-start(bf16[2,128,512]{2,1,0:T(8,128)(2,1)S(1)} %get-tuple-element.38), channel_id=1, source_target_pairs={{0,8},{4,12},{8,0},{12,4},{16,24},{20,28},{24,16},{28,20},{1,9},{5... | collective-permute-start | bytes 786440 | tf_op jit(solution)/shard_map/ppermute | solution.py:18
  92.7 7.8 %input_terms.1 = (bf16[2,256,1024]{2,1,0:T(8,128)(2,1)}, f32[2,256,1024]{2,1,0:T(8,128)}) custom-call(s32[8]{0:T(128)} %broadcast_xor_fusion.1.order_ref, bf16[4,128,1024]{2,1,0:T(8,128)(2,1)} %pad_maximum_fusion.refs_0_, bf16[4,128,1024]{2,1,0:T(8,128)(2,1)} %collective-permute-done.2.refs_1_, bf16[256,512]{1,0:T(8,128)(2,1)} %get-tuple-element.22.refs_2_.refs_8_, ...), custom_call_target="tpu_custom_call" | custom-call | flops 2147483648 | bytes 5242880 | tf_op jit(solution)/shard_map/input_terms/pallas_call | solution.py:220
  101.5 1.5 %add_convert_fusion.2 = (bf16[2,128,512]{2,1,0:T(8,128)(2,1)S(1)}, f32[2,128,512]{2,1,0:T(8,128)S(1)}) fusion(f32[4,128,512]{2,1,0:T(8,128)} %get-tuple-element.34, bf16[4,128,512]{2,1,0:T(8,128)(2,1)} %collective-permute-done.17), kind=kLoop, calls=%fused_computation.5 | loop fusion | flops 655360 | bytes 2359296 | tf_op jit(solution)/shard_map/convert_element_type | solution.py:348
  103.0 1.5 %collective-permute-start.18 = (bf16[2,128,512]{2,1,0:T(8,128)(2,1)S(1)}, bf16[2,128,512]{2,1,0:T(8,128)(2,1)S(1)}, u32[]{:S(2)}, u32[]{:S(2)}) collective-permute-start(bf16[2,128,512]{2,1,0:T(8,128)(2,1)S(1)} %get-tuple-element.36), channel_id=1, source_target_pairs={{0,8},{4,12},{8,0},{12,4},{16,24},{20,28},{24,16},{28,20},{1,9},{5... | collective-permute-start | bytes 786440 | tf_op jit(solution)/shard_map/ppermute | solution.py:18
  106.8 6.6 %collective-permute-done.18 = bf16[2,128,512]{2,1,0:T(8,128)(2,1)S(1)} collective-permute-done((bf16[2,128,512]{2,1,0:T(8,128)(2,1)S(1)}, bf16[2,128,512]{2,1,0:T(8,128)(2,1)S(1)}, u32[]{:S(2)}, u32[]{:S(2)}) %collective-permute-start.18) | collective-permute-done | bytes 262176 | tf_op jit(solution)/shard_map/ppermute | solution.py:18
  114.0 1.3 collective-permute-done.16
  117.3 1.1 add_convert_fusion.1
  118.4 1.0 collective-permute-start.10
  119.5 2.3 %collective-permute-done.19 = bf16[1,128,512]{2,1,0:T(8,128)(2,1)S(1)} collective-permute-done((bf16[1,128,512]{2,1,0:T(8,128)(2,1)S(1)}, bf16[1,128,512]{2,1,0:T(8,128)(2,1)S(1)}, u32[]{:S(2)}, u32[]{:S(2)}) %collective-permute-start.19) | collective-permute-done | bytes 131104 | tf_op jit(solution)/shard_map/ppermute | solution.py:18
  123.5 10.6 %collective-permute-done.23.refs_5_ = bf16[128,512]{1,0:T(8,128)(2,1)S(1)} collective-permute-done((bf16[128,512]{1,0:T(8,128)(2,1)S(1)}, bf16[128,512]{1,0:T(8,128)(2,1)S(1)}, u32[]{:S(2)}, u32[]{:S(2)}) %collective-permute-start.23) | collective-permute-done | bytes 131104 | tf_op jit(solution)/shard_map/ppermute | solution.py:18
  136.2 3.8 %place_units.1 = f32[128,4096]{1,0:T(8,128)} custom-call(s32[4]{0:T(128)} %iota_xor_fusion.order_ref, bf16[128,512]{1,0:T(8,128)(2,1)} %copy-done.12, bf16[128,512]{1,0:T(8,128)(2,1)} %copy-done.13, bf16[128,512]{1,0:T(8,128)(2,1)} %copy-done.18, bf16[128,512]{1,0:T(8,128)(2,1)} %copy-done.19, bf16[128,512]{1,0:T(8,128)(2,1)} %copy-done.16, ...), custom_call_target="tpu_custom_call" | custom-call | flops 524288 | bytes 3145728 | tf_op jit(solution)/shard_map/place_units/pallas_call | solution.py:254
  140.0 2.2 %fusion = bf16[256,1024]{1,0:T(8,128)(2,1)} fusion(bf16[1,256,1024]{2,1,0:T(8,128)(2,1)} %collective-permute-done.10, f32[2,256,1024]{2,1,0:T(8,128)S(1)} %copy-done.7, bf16[2,256,1024]{2,1,0:T(8,128)(2,1)} %copy-done.9), kind=kLoop, calls=%fused_computation.3 | loop fusion | flops 1310720 | bytes 2621440 | tf_op jit(solution)/shard_map/convert_element_type | solution.py:376
  (99 shorter events, 21.5 us)
Async XLA Ops:
  1.9 16.1 %collective-permute-start = (bf16[1,128,1024]{2,1,0:T(8,128)(2,1)S(1)}, bf16[1,128,1024]{2,1,0:T(8,128)(2,1)S(1)}, u32[]{:S(2)}, u32[]{:S(2)}) collective-permute-start(bf16[1,128,1024]{2,1,0:T(8,128)(2,1)S(1)} %dynamic-slice_bitcast_fusion), channel_id=1, source_target_pairs={{0,16},{4,20},{8,24},{12,28},{16,0},{20,4},{24,8},{28,12},{1,17},{... | collective-permute-start | bytes 786440 | tf_op jit(solution)/shard_map/ppermute | solution.py:18
  6.0 47.3 %collective-permute-start.12 = (bf16[256,1024]{1,0:T(8,128)(2,1)}, bf16[256,1024]{1,0:T(8,128)(2,1)S(1)}, u32[]{:S(2)}, u32[]{:S(2)}) collective-permute-start(bf16[256,1024]{1,0:T(8,128)(2,1)} %refs_4_.3), channel_id=1, source_target_pairs={{0,2},{1,3},{2,0},{3,1},{4,6},{5,7},{6,4},{7,5},{8,10},{9,11},{10,... | collective-permute-start | bytes 1572872 | tf_op jit(solution)/shard_map/ppermute | solution.py:18
  19.5 39.5 %collective-permute-start.1 = (bf16[2,128,1024]{2,1,0:T(8,128)(2,1)}, bf16[2,128,1024]{2,1,0:T(8,128)(2,1)}, u32[]{:S(2)}, u32[]{:S(2)}) collective-permute-start(bf16[2,128,1024]{2,1,0:T(8,128)(2,1)} %pad_maximum_fusion.1), channel_id=1, source_target_pairs={{0,4},{4,0},{8,12},{12,8},{16,20},{20,16},{24,28},{28,24},{1,5},{5... | collective-permute-start | bytes 1572872 | tf_op jit(solution)/shard_map/ppermute | solution.py:18
  26.6 12.1 %all-to-all-start = ((f32[64,1,128]{2,1,0:T(1,128)}), f32[64,1,128]{2,1,0:T(1,128)S(1)}, u32[]{:S(2)}, u32[]{:S(2)}) async-start(f32[64,1,128]{2,1,0:T(1,128)} %get-tuple-element.21), calls=%async_computation | async-start | bytes 65536 | tf_op jit(solution)/shard_map/all_to_all | solution.py:274
  39.3 9.8 %all-to-all-start.1 = ((f32[64,1,128]{2,1,0:T(1,128)}), f32[64,1,128]{2,1,0:T(1,128)S(1)}, u32[]{:S(2)}, u32[]{:S(2)}) async-start(f32[64,1,128]{2,1,0:T(1,128)} %bitcast.6), calls=%async_computation.1 | async-start | bytes 65536 | tf_op jit(solution)/shard_map/all_to_all | solution.py:277
  52.8 10.0 %collective-permute-start.3 = (bf16[256,512]{1,0:T(8,128)(2,1)}, bf16[256,512]{1,0:T(8,128)(2,1)}, u32[]{:S(2)}, u32[]{:S(2)}) collective-permute-start(bf16[256,512]{1,0:T(8,128)(2,1)} %get-tuple-element.24), channel_id=1, source_target_pairs={{0,2},{1,3},{2,0},{3,1},{4,6},{5,7},{6,4},{7,5},{8,10},{9,11},{10,... | collective-permute-start | bytes 786440 | tf_op jit(solution)/shard_map/ppermute | solution.py:18
  53.3 14.7 %collective-permute-start.11 = (bf16[256,1024]{1,0:T(8,128)(2,1)S(1)}, bf16[256,1024]{1,0:T(8,128)(2,1)S(1)}, u32[]{:S(2)}, u32[]{:S(2)}) collective-permute-start(bf16[256,1024]{1,0:T(8,128)(2,1)S(1)} %copy-done.1), channel_id=1, source_target_pairs={{0,1},{1,0},{2,3},{3,2},{4,5},{5,4},{6,7},{7,6},{8,9},{9,8},{10,11... | collective-permute-start | bytes 1572872 | tf_op jit(solution)/shard_map/ppermute | solution.py:18
  53.3 16.3 %collective-permute-start.13 = (bf16[256,1024]{1,0:T(8,128)(2,1)S(1)}, bf16[256,1024]{1,0:T(8,128)(2,1)S(1)}, u32[]{:S(2)}, u32[]{:S(2)}) collective-permute-start(bf16[256,1024]{1,0:T(8,128)(2,1)S(1)} %collective-permute-done.12.refs_2_.refs_6_), channel_id=1, source_target_pairs={{0,1},{1,0},{2,3},{3,2},{4,5},{5,4},{6,7},{7,6},{8,9},{9,8},{10,11... | collective-permute-start | bytes 1572872 | tf_op jit(solution)/shard_map/ppermute | solution.py:18
  58.8 8.6 %collective-permute-start.5 = (bf16[256,512]{1,0:T(8,128)(2,1)}, bf16[256,512]{1,0:T(8,128)(2,1)}, u32[]{:S(2)}, u32[]{:S(2)}) collective-permute-start(bf16[256,512]{1,0:T(8,128)(2,1)} %get-tuple-element.26), channel_id=1, source_target_pairs={{0,1},{1,0},{2,3},{3,2},{4,5},{5,4},{6,7},{7,6},{8,9},{9,8},{10,11... | collective-permute-start | bytes 786440 | tf_op jit(solution)/shard_map/ppermute | solution.py:18
  59.0 9.0 %collective-permute-start.7 = (bf16[256,512]{1,0:T(8,128)(2,1)}, bf16[256,512]{1,0:T(8,128)(2,1)}, u32[]{:S(2)}, u32[]{:S(2)}) collective-permute-start(bf16[256,512]{1,0:T(8,128)(2,1)} %get-tuple-element.28), channel_id=1, source_target_pairs={{0,3},{1,2},{2,1},{3,0},{4,7},{5,6},{6,5},{7,4},{8,11},{9,10},{10,... | collective-permute-start | bytes 786440 | tf_op jit(solution)/shard_map/ppermute | solution.py:18
  62.8 29.9 %collective-permute-start.2 = (bf16[4,128,1024]{2,1,0:T(8,128)(2,1)}, bf16[4,128,1024]{2,1,0:T(8,128)(2,1)}, u32[]{:S(2)}, u32[]{:S(2)}) collective-permute-start(bf16[4,128,1024]{2,1,0:T(8,128)(2,1)} %pad_maximum_fusion.refs_0_), channel_id=1, source_target_pairs={{0,8},{4,12},{8,0},{12,4},{16,24},{20,28},{24,16},{28,20},{1,9},{5... | collective-permute-start | bytes 3145736 | tf_op jit(solution)/shard_map/ppermute | solution.py:18
  67.4 9.4 %collective-permute-start.4 = (bf16[256,512]{1,0:T(8,128)(2,1)}, bf16[256,512]{1,0:T(8,128)(2,1)S(1)}, u32[]{:S(2)}, u32[]{:S(2)}) collective-permute-start(bf16[256,512]{1,0:T(8,128)(2,1)} %get-tuple-element.25), channel_id=1, source_target_pairs={{0,2},{1,3},{2,0},{3,1},{4,6},{5,7},{6,4},{7,5},{8,10},{9,11},{10,... | collective-permute-start | bytes 786440 | tf_op jit(solution)/shard_map/ppermute | solution.py:18
  68.0 8.9 %collective-permute-start.6 = (bf16[256,512]{1,0:T(8,128)(2,1)}, bf16[256,512]{1,0:T(8,128)(2,1)}, u32[]{:S(2)}, u32[]{:S(2)}) collective-permute-start(bf16[256,512]{1,0:T(8,128)(2,1)} %get-tuple-element.27), channel_id=1, source_target_pairs={{0,1},{1,0},{2,3},{3,2},{4,5},{5,4},{6,7},{7,6},{8,9},{9,8},{10,11... | collective-permute-start | bytes 786440 | tf_op jit(solution)/shard_map/ppermute | solution.py:18
  68.0 12.1 %collective-permute-start.8 = (bf16[256,512]{1,0:T(8,128)(2,1)}, bf16[256,512]{1,0:T(8,128)(2,1)S(1)}, u32[]{:S(2)}, u32[]{:S(2)}) collective-permute-start(bf16[256,512]{1,0:T(8,128)(2,1)} %get-tuple-element.29), channel_id=1, source_target_pairs={{0,3},{1,2},{2,1},{3,0},{4,7},{5,6},{6,5},{7,4},{8,11},{9,10},{10,... | collective-permute-start | bytes 786440 | tf_op jit(solution)/shard_map/ppermute | solution.py:18
  76.1 14.2 %collective-permute-start.14 = (bf16[4,128,512]{2,1,0:T(8,128)(2,1)}, bf16[4,128,512]{2,1,0:T(8,128)(2,1)S(1)}, u32[]{:S(2)}, u32[]{:S(2)}) collective-permute-start(bf16[4,128,512]{2,1,0:T(8,128)(2,1)} %get-tuple-element.33), channel_id=1, source_target_pairs={{0,4},{4,0},{8,12},{12,8},{16,20},{20,16},{24,28},{28,24},{1,5},{5... | collective-permute-start | bytes 1572872 | tf_op jit(solution)/shard_map/ppermute | solution.py:18
  86.7 14.8 %collective-permute-start.17 = (bf16[4,128,512]{2,1,0:T(8,128)(2,1)}, bf16[4,128,512]{2,1,0:T(8,128)(2,1)}, u32[]{:S(2)}, u32[]{:S(2)}) collective-permute-start(bf16[4,128,512]{2,1,0:T(8,128)(2,1)} %get-tuple-element.35), channel_id=1, source_target_pairs={{0,4},{4,0},{8,12},{12,8},{16,20},{20,16},{24,28},{28,24},{1,5},{5... | collective-permute-start | bytes 1572872 | tf_op jit(solution)/shard_map/ppermute | solution.py:18
  91.3 13.8 %collective-permute-start.15 = (bf16[2,128,512]{2,1,0:T(8,128)(2,1)S(1)}, bf16[2,128,512]{2,1,0:T(8,128)(2,1)}, u32[]{:S(2)}, u32[]{:S(2)}) collective-permute-start(bf16[2,128,512]{2,1,0:T(8,128)(2,1)S(1)} %get-tuple-element.38), channel_id=1, source_target_pairs={{0,8},{4,12},{8,0},{12,4},{16,24},{20,28},{24,16},{28,20},{1,9},{5... | collective-permute-start | bytes 786440 | tf_op jit(solution)/shard_map/ppermute | solution.py:18
  100.6 14.7 %copy-start.8 = (f32[2,128,512]{2,1,0:T(8,128)S(1)}, f32[2,128,512]{2,1,0:T(8,128)}, u32[]{:S(2)}) copy-start(f32[2,128,512]{2,1,0:T(8,128)} %get-tuple-element.39) | copy-start | bytes 1572868
  100.6 16.7 %copy-start.7 = (f32[2,256,1024]{2,1,0:T(8,128)S(1)}, f32[2,256,1024]{2,1,0:T(8,128)}, u32[]{:S(2)}) copy-start(f32[2,256,1024]{2,1,0:T(8,128)} %get-tuple-element.30) | copy-start | bytes 6291460
  100.6 16.7 %collective-permute-start.9 = (bf16[2,256,1024]{2,1,0:T(8,128)(2,1)}, bf16[2,256,1024]{2,1,0:T(8,128)(2,1)S(1)}, u32[]{:S(2)}, u32[]{:S(2)}) collective-permute-start(bf16[2,256,1024]{2,1,0:T(8,128)(2,1)} %get-tuple-element.31), channel_id=1, source_target_pairs={{0,1},{1,0},{2,3},{3,2},{4,5},{5,4},{6,7},{7,6},{8,9},{9,8},{10,11... | collective-permute-start | bytes 3145736 | tf_op jit(solution)/shard_map/ppermute | solution.py:18
  103.0 10.4 %collective-permute-start.18 = (bf16[2,128,512]{2,1,0:T(8,128)(2,1)S(1)}, bf16[2,128,512]{2,1,0:T(8,128)(2,1)S(1)}, u32[]{:S(2)}, u32[]{:S(2)}) collective-permute-start(bf16[2,128,512]{2,1,0:T(8,128)(2,1)S(1)} %get-tuple-element.36), channel_id=1, source_target_pairs={{0,8},{4,12},{8,0},{12,4},{16,24},{20,28},{24,16},{28,20},{1,9},{5... | collective-permute-start | bytes 786440 | tf_op jit(solution)/shard_map/ppermute | solution.py:18
  106.1 16.7 %copy-start.6 = (f32[64,1,128]{2,1,0:T(1,128)S(1)}, f32[64,1,128]{2,1,0:T(1,128)}, u32[]{:S(2)}) copy-start(f32[64,1,128]{2,1,0:T(1,128)} %copy-done.5) | copy-start | bytes 98308
  106.1 9.2 %collective-permute-start.16 = (bf16[1,128,512]{2,1,0:T(8,128)(2,1)S(1)}, bf16[1,128,512]{2,1,0:T(8,128)(2,1)S(1)}, u32[]{:S(2)}, u32[]{:S(2)}) collective-permute-start(bf16[1,128,512]{2,1,0:T(8,128)(2,1)S(1)} %fusion.4), channel_id=1, source_target_pairs={{0,16},{4,20},{8,24},{12,28},{16,0},{20,4},{24,8},{28,12},{1,17},{... | collective-permute-start | bytes 393224 | tf_op jit(solution)/shard_map/ppermute | solution.py:18
  113.4 8.3 %collective-permute-start.19 = (bf16[1,128,512]{2,1,0:T(8,128)(2,1)S(1)}, bf16[1,128,512]{2,1,0:T(8,128)(2,1)S(1)}, u32[]{:S(2)}, u32[]{:S(2)}) collective-permute-start(bf16[1,128,512]{2,1,0:T(8,128)(2,1)S(1)} %fusion.1), channel_id=1, source_target_pairs={{0,16},{4,20},{8,24},{12,28},{16,0},{20,4},{24,8},{28,12},{1,17},{... | collective-permute-start | bytes 393224 | tf_op jit(solution)/shard_map/ppermute | solution.py:18
  116.2 19.9 %copy-start.12 = (bf16[128,512]{1,0:T(8,128)(2,1)}, bf16[128,512]{1,0:T(8,128)(2,1)S(1)}, u32[]{:S(2)}) copy-start(bf16[128,512]{1,0:T(8,128)(2,1)S(1)} %fusion.7.refs_0_) | copy-start | bytes 393220
  116.3 7.2 %collective-permute-start.22 = (bf16[128,512]{1,0:T(8,128)(2,1)S(1)}, bf16[128,512]{1,0:T(8,128)(2,1)S(1)}, u32[]{:S(2)}, u32[]{:S(2)}) collective-permute-start(bf16[128,512]{1,0:T(8,128)(2,1)S(1)} %fusion.7.refs_0_), channel_id=1, source_target_pairs={{0,2},{1,3},{2,0},{3,1},{4,6},{5,7},{6,4},{7,5},{8,10},{9,11},{10,... | collective-permute-start | bytes 393224 | tf_op jit(solution)/shard_map/ppermute | solution.py:18
  118.4 21.6 %collective-permute-start.10 = (bf16[1,256,1024]{2,1,0:T(8,128)(2,1)}, bf16[1,256,1024]{2,1,0:T(8,128)(2,1)}, u32[]{:S(2)}, u32[]{:S(2)}) collective-permute-start(bf16[1,256,1024]{2,1,0:T(8,128)(2,1)} %add_convert_fusion.1), channel_id=1, source_target_pairs={{0,2},{1,3},{2,0},{3,1},{4,6},{5,7},{6,4},{7,5},{8,10},{9,11},{10,... | collective-permute-start | bytes 1572872 | tf_op jit(solution)/shard_map/ppermute | solution.py:18
  121.8 12.3 %collective-permute-start.23 = (bf16[128,512]{1,0:T(8,128)(2,1)S(1)}, bf16[128,512]{1,0:T(8,128)(2,1)S(1)}, u32[]{:S(2)}, u32[]{:S(2)}) collective-permute-start(bf16[128,512]{1,0:T(8,128)(2,1)S(1)} %fusion.8.refs_1_), channel_id=1, source_target_pairs={{0,2},{1,3},{2,0},{3,1},{4,6},{5,7},{6,4},{7,5},{8,10},{9,11},{10,... | collective-permute-start | bytes 393224 | tf_op jit(solution)/shard_map/ppermute | solution.py:18
  122.8 12.0 %collective-permute-start.20 = (bf16[128,512]{1,0:T(8,128)(2,1)S(1)}, bf16[128,512]{1,0:T(8,128)(2,1)S(1)}, u32[]{:S(2)}, u32[]{:S(2)}) collective-permute-start(bf16[128,512]{1,0:T(8,128)(2,1)S(1)} %fusion.7.refs_0_), channel_id=1, source_target_pairs={{0,1},{1,0},{2,3},{3,2},{4,5},{5,4},{6,7},{7,6},{8,9},{9,8},{10,11... | collective-permute-start | bytes 393224 | tf_op jit(solution)/shard_map/ppermute | solution.py:18
  122.9 11.9 %collective-permute-start.21 = (bf16[128,512]{1,0:T(8,128)(2,1)S(1)}, bf16[128,512]{1,0:T(8,128)(2,1)S(1)}, u32[]{:S(2)}, u32[]{:S(2)}) collective-permute-start(bf16[128,512]{1,0:T(8,128)(2,1)S(1)} %fusion.8.refs_1_), channel_id=1, source_target_pairs={{0,1},{1,0},{2,3},{3,2},{4,5},{5,4},{6,7},{7,6},{8,9},{9,8},{10,11... | collective-permute-start | bytes 393224 | tf_op jit(solution)/shard_map/ppermute | solution.py:18
  123.4 11.4 %collective-permute-start.24 = (bf16[128,512]{1,0:T(8,128)(2,1)S(1)}, bf16[128,512]{1,0:T(8,128)(2,1)S(1)}, u32[]{:S(2)}, u32[]{:S(2)}) collective-permute-start(bf16[128,512]{1,0:T(8,128)(2,1)S(1)} %collective-permute-done.22.refs_4_), channel_id=1, source_target_pairs={{0,1},{1,0},{2,3},{3,2},{4,5},{5,4},{6,7},{7,6},{8,9},{9,8},{10,11... | collective-permute-start | bytes 393224 | tf_op jit(solution)/shard_map/ppermute | solution.py:18
  134.1 2.0 %collective-permute-start.25 = (bf16[128,512]{1,0:T(8,128)(2,1)S(1)}, bf16[128,512]{1,0:T(8,128)(2,1)}, u32[]{:S(2)}, u32[]{:S(2)}) collective-permute-start(bf16[128,512]{1,0:T(8,128)(2,1)S(1)} %collective-permute-done.23.refs_5_), channel_id=1, source_target_pairs={{0,1},{1,0},{2,3},{3,2},{4,5},{5,4},{6,7},{7,6},{8,9},{9,8},{10,11... | collective-permute-start | bytes 393224 | tf_op jit(solution)/shard_map/ppermute | solution.py:18
  (19 other events, 73.8 us)
